TPU v7x, 128 devices: a whole 4x4x4 slice. The times are simulated.
128 devices in a mesh: grp: 4 (over x), dev: 32 (over z, y, core).
Axes of the slice: x: 4, y: 4, z: 4, core: 2. Of those that a mesh axis runs over, the one named last changes fastest.
Arguments:
- embeddings: bfloat16 [1048576, 256], P(('grp', 'dev'))
- prior_dist: float32 [1048576], P(('grp', 'dev')), may hold values from 1 to 3
- seed_ids: int32 [6, 512], replicated, may hold values from 0 to 1048575, as said below
Outputs:
- min_dist: float32 [1048576], P(('grp', 'dev'))
- group_means: float32 [6, 4], P(None, 'grp')
Inputs may be any that keep to these rules, and one draw needn't show every extreme that they name: `seed_ids`: round r's ids all lie in the rows of group r mod 4, that is from (r mod 4) * 262144 to (r mod 4 + 1) * 262144 - 1; ids may repeat.
All inputs are finite; a program needn't handle non-finite values.
Results may differ from a plain program's by a relative error of at most 0.0003.
Values may be sent and summed in bfloat16 or wider, within the bound.
A program may use at most 64 MiB of HBM per device.

v0:
```python
import jax
import jax.numpy as jnp
from jax import lax
from jax.sharding import PartitionSpec as P


def from_everyone(value, axis):
    copies = jnp.broadcast_to(value, (lax.axis_size(axis), *value.shape))
    return lax.all_to_all(copies, axis, split_axis=0, concat_axis=0, tiled=True)


def of_everyone(value, axis):
    everything = from_everyone(value, axis)
    return jnp.sum(everything, axis=0)


def block_gaps(block, block_norms, centers, seed_norms, feature_dim):
    products = jnp.dot(block, centers.T, preferred_element_type=jnp.float32)
    return jnp.maximum(block_norms[:, None] + seed_norms[None, :] - 2.0 * products, 0.0) / float(
        feature_dim
    )


def body(embeddings, prior_dist, seed_ids):
    row_count, feature_dim = embeddings.shape
    round_count, seed_count = seed_ids.shape
    dev_count = lax.axis_size("dev")
    row_start = (lax.axis_index("grp") * dev_count + lax.axis_index("dev")) * row_count
    offsets = seed_ids - row_start
    inside = (offsets >= 0) & (offsets < row_count)
    picked = jnp.take(embeddings, jnp.clip(offsets, 0, row_count - 1), axis=0)
    picked = jnp.where(inside[:, :, None], picked.astype(jnp.float32), 0.0)
    owned = lax.psum(picked.astype(jnp.bfloat16), "dev")
    summed = lax.psum(owned, "grp")
    centers = [summed[round_index] for round_index in range(round_count)]
    seed_norms = [jnp.sum(jnp.square(center.astype(jnp.float32)), axis=1) for center in centers]
    row_norms = jnp.sum(jnp.square(embeddings.astype(jnp.float32)), axis=1)
    block_rows = min(2048, row_count)
    block_count = row_count // block_rows
    blocks = embeddings.reshape(block_count, block_rows, feature_dim)
    norm_blocks = row_norms.reshape(block_count, block_rows)
    per_round = []
    for round_index in range(round_count):
        center = centers[round_index]
        center_norms = seed_norms[round_index]

        def one_round(pair, center=center, center_norms=center_norms):
            return jnp.min(block_gaps(pair[0], pair[1], center, center_norms, feature_dim), axis=1)

        per_round.append(lax.map(one_round, (blocks, norm_blocks)).reshape(row_count))
    group_total = float(row_count * dev_count)
    current = prior_dist
    partial_value = []
    for round_index in range(round_count):
        current = jnp.minimum(current, per_round[round_index])
        partial_value.append(jnp.sum(current))
    summed_totals = of_everyone(jnp.stack(partial_value), "dev")
    means = summed_totals / group_total
    return (current, means.reshape(round_count, 1))


def solution(mesh):
    placed = (P(("grp", "dev"), None), P(("grp", "dev")), P())
    return jax.shard_map(
        body,
        mesh=mesh,
        in_specs=placed,
        out_specs=(P(("grp", "dev")), P(None, "grp")),
        check_vma=False,
    )
```

profile of v0, /device:TPU:1, one launch (start us, length us, event | category | flops | bytes accessed | tf_op | source)
XLA Modules:
  0.0 274.7 jit_solution(4670967957173389991)
XLA Ops:
  7.2 0.7 compare_and_fusion
  8.0 12.5 %gather_fusion = bf16[3072,256]{1,0:T(8,128)(2,1)S(1)} fusion(bf16[8192,256]{1,0:T(8,128)(2,1)} %param.15, s32[3072]{0:T(1024)S(1)} %broadcast_clamp_fusion), kind=kCustom, calls=%fused_computation | custom fusion | bytes 3158016 | tf_op jit(solution)/shard_map/jit(_take)/gather | solution.py:31
  20.5 2.4 select_convert_fusion
  23.0 109.9 %all-reduce.3.cloned.1.call-done = bf16[6,512,256]{2,1,0:T(8,128)(2,1)} async-done(((bf16[6,512,256]{2,1,0:T(8,128)(2,1)}), bf16[6,512,256]{2,1,0:T(8,128)(2,1)}) %all-reduce.3.cloned.1.call-update) | async-done | bytes 1572880 | tf_op jit(solution)/shard_map/psum | solution.py:33
  133.0 3.3 %multiply_reduce_fusion.6 = f32[8192]{0:T(1024)S(1)} fusion(bf16[8192,256]{1,0:T(8,128)(2,1)} %param.15), kind=kLoop, calls=%fused_computation.31 | loop fusion | flops 6283264 | bytes 4227072 | tf_op jit(solution)/shard_map/reduce_sum | solution.py:37
  136.3 48.8 %all-reduce.5.cloned.1.call-done = bf16[6,512,256]{2,1,0:T(8,128)(2,1)} async-done(((bf16[6,512,256]{2,1,0:T(8,128)(2,1)}), bf16[6,512,256]{2,1,0:T(8,128)(2,1)}) %all-reduce.5.cloned.1.call-update) | async-done | bytes 1572880 | tf_op jit(solution)/shard_map/psum | solution.py:34
  185.1 1.6 slice_bitcast_fusion.5
  186.7 0.3 copy-done
  187.0 0.5 multiply_reduce_fusion.8
  187.5 9.9 %while.62 = (s32[]{:T(128)}, f32[4,2048]{1,0:T(4,128)S(1)}, f32[4,2048]{1,0:T(4,128)S(1)}, f32[512]{0:T(512)S(1)}, bf16[4,2048,256]{2,1,0:T(8,128)(2,1)}, /*inde...) while((s32[]{:T(128)}, f32[4,2048]{1,0:T(4,128)S(1)}, f32[4,2048]{1,0:T(4,128)S(1)}, f32[512]{0:T(512)S(1)}, ...), condition=%wide.region_14.15_spmd, body=%wide.region_12.14_spmd.sunk | while | flops 543160320 | bytes 1362525 | solution.py:50
  187.6 2.3 multiply_reduce_fusion.21
  189.9 0.1 dynamic_update_slice.27
  190.0 2.3 multiply_reduce_fusion.21
  192.3 0.1 dynamic_update_slice.27
  192.5 2.3 multiply_reduce_fusion.21
  194.8 0.1 dynamic_update_slice.27
  195.0 2.3 multiply_reduce_fusion.21
  197.3 0.1 dynamic_update_slice.27
  197.4 9.9 %while.64 = (s32[]{:T(128)}, f32[4,2048]{1,0:T(4,128)S(1)}, f32[4,2048]{1,0:T(4,128)S(1)}, f32[512]{0:T(512)S(1)}, bf16[4,2048,256]{2,1,0:T(8,128)(2,1)}, /*inde...) while((s32[]{:T(128)}, f32[4,2048]{1,0:T(4,128)S(1)}, f32[4,2048]{1,0:T(4,128)S(1)}, f32[512]{0:T(512)S(1)}, ...), condition=%wide.region_22.23_spmd, body=%wide.region_20.22_spmd.sunk | while | flops 543160320 | bytes 1362525 | solution.py:50
  197.5 2.3 multiply_reduce_fusion.23
  199.9 2.3 multiply_reduce_fusion.23
  202.4 2.3 multiply_reduce_fusion.23
  204.9 2.3 multiply_reduce_fusion.23
  207.3 9.9 %while.60 = (s32[]{:T(128)}, f32[4,2048]{1,0:T(4,128)S(1)}, f32[4,2048]{1,0:T(4,128)S(1)}, f32[512]{0:T(512)S(1)}, bf16[4,2048,256]{2,1,0:T(8,128)(2,1)}, /*inde...) while((s32[]{:T(128)}, f32[4,2048]{1,0:T(4,128)S(1)}, f32[4,2048]{1,0:T(4,128)S(1)}, f32[512]{0:T(512)S(1)}, ...), condition=%wide.region_6.7_spmd, body=%wide.region_4.6_spmd.sunk | while | flops 543160320 | bytes 1362525 | solution.py:50
  207.4 2.3 multiply_reduce_fusion.19
  209.8 2.3 multiply_reduce_fusion.19
  212.3 2.3 multiply_reduce_fusion.19
  214.8 2.3 multiply_reduce_fusion.19
  217.2 9.9 %while.61 = (s32[]{:T(128)}, f32[4,2048]{1,0:T(4,128)S(1)}, f32[4,2048]{1,0:T(4,128)S(1)}, f32[512]{0:T(512)S(1)}, bf16[4,2048,256]{2,1,0:T(8,128)(2,1)}, /*inde...) while((s32[]{:T(128)}, f32[4,2048]{1,0:T(4,128)S(1)}, f32[4,2048]{1,0:T(4,128)S(1)}, f32[512]{0:T(512)S(1)}, ...), condition=%wide.region_10.11_spmd, body=%wide.region_8.10_spmd.sunk | while | flops 543160320 | bytes 1362525 | solution.py:50
  217.3 2.3 multiply_reduce_fusion.20
  219.7 2.3 multiply_reduce_fusion.20
  222.2 2.3 multiply_reduce_fusion.20
  224.6 2.3 multiply_reduce_fusion.20
  227.1 9.8 %while.63 = (s32[]{:T(128)}, f32[4,2048]{1,0:T(4,128)S(1)}, f32[4,2048]{1,0:T(4,128)S(1)}, f32[512]{0:T(512)S(1)}, bf16[4,2048,256]{2,1,0:T(8,128)(2,1)}, /*inde...) while((s32[]{:T(128)}, f32[4,2048]{1,0:T(4,128)S(1)}, f32[4,2048]{1,0:T(4,128)S(1)}, f32[512]{0:T(512)S(1)}, ...), condition=%wide.region_18.19_spmd, body=%wide.region_16.18_spmd.sunk | while | flops 543160320 | bytes 1362525 | solution.py:50
  227.1 2.3 multiply_reduce_fusion.22
  229.6 2.3 multiply_reduce_fusion.22
  232.1 2.3 multiply_reduce_fusion.22
  234.5 2.3 multiply_reduce_fusion.22
  237.0 9.8 %while.65 = (s32[]{:T(128)}, f32[4,2048]{1,0:T(4,128)S(1)}, f32[4,2048]{1,0:T(4,128)S(1)}, f32[512]{0:T(512)S(1)}, bf16[4,2048,256]{2,1,0:T(8,128)(2,1)}, /*inde...) while((s32[]{:T(128)}, f32[4,2048]{1,0:T(4,128)S(1)}, f32[4,2048]{1,0:T(4,128)S(1)}, f32[512]{0:T(512)S(1)}, ...), condition=%wide.region_26.27_spmd, body=%wide.region_24.26_spmd.sunk | while | flops 543160320 | bytes 1362525 | solution.py:50
  237.0 2.3 multiply_reduce_fusion.24
  239.5 2.3 multiply_reduce_fusion.24
  241.9 2.3 multiply_reduce_fusion.24
  244.4 2.3 multiply_reduce_fusion.24
  246.9 1.3 fusion.18
  248.2 0.7 minimum_reduce_fusion
  248.9 3.8 %stack.27 = f32[6]{0:T(128)S(1)} concatenate(f32[1]{0:T(128)} %bitcast.26, f32[1]{0:T(128)} %bitcast.27, f32[1]{0:T(128)} %bitcast.28, f32[1]{0:T(128)} %bitcast.29, f32[1]{0:T(128)} %bitcast.30, f32[1]{0:T(128)} %bitcast.31), dimensions={0} | concatenate | bytes 48 | tf_op jit(solution)/shard_map/stack | solution.py:57
  252.7 14.6 %all_to_all.6 = f32[32,1,6]{2,1,0:T(1,128)S(1)} all-to-all(f32[32,1,6]{2,1,0:T(1,128)S(1)} %broadcast_in_dim.64), channel_id=1, replica_groups=mesh['grp'=4,'dev'=32] {'dev'}, dimensions={0} | all-to-all | bytes 1536 | tf_op jit(solution)/shard_map/all_to_all | solution.py:9
  267.4 0.5 multiply_bitcast_fusion
  (68 shorter events, 3.1 us)
Async XLA Ops:
  7.2 125.8 %all-reduce.3.cloned.1.call-start = ((), (), s32[]{:S(2)}) async-start(), calls=%async_computation.1 | async-start | bytes 3145728 | tf_op jit(solution)/shard_map/psum | solution.py:33
  22.9 162.2 %all-reduce.5.cloned.1.call-start = ((), (), s32[]{:S(2)}) async-start(), calls=%async_computation.2 | async-start | bytes 3145728 | tf_op jit(solution)/shard_map/psum | solution.py:34
  185.1 1.9 copy-start
  237.0 9.9 %copy-start.1 = (f32[8192]{0:T(1024)S(1)}, f32[8192]{0:T(1024)}, u32[]{:S(2)}) copy-start(f32[8192]{0:T(1024)} %param.16) | copy-start | bytes 98308
Sparse Core Ops, SparseCore 0:
  23.1 109.8 all-reduce.2
  135.3 49.8 all-reduce.4
where the time goes:
time: 276 us; the launch traced here: 275 us
  waiting for transfers between devices  159 us (58%)
  matrix products  54.8 us (20%)
  local copies, waits for them, and re-layouts  21.8 us (8%)
  blocking collectives  14.6 us (5%)
  between operations  14.2 us (5%)
  other arithmetic  9.52 us (3%)
    psum x1, waiting for transfers between devices, body(): owned = lax.psum(picked.astype(jnp.bfloat16), 'dev')  110 us
    dot_general x24, matrix products, block_gaps(): products = jnp.dot(block, centers.T, preferred_element_type=jnp.float32)  54.8 us
    psum x1, waiting for transfers between devices, body(): summed = lax.psum(owned, 'grp')  48.8 us
    all_to_all x1, blocking collectives, from_everyone(): return lax.all_to_all(copies, axis, split_axis=0, concat_axis=0, tiled=True)  14.6 us
    gather x1, local copies, waits for them, and re-layouts, body(): picked = jnp.take(embeddings, jnp.clip(offsets, 0, row_count - 1), axis=0)  12.5 us
  transfers between devices with their start and end apart: 2, of which 2 were waited for; matrix products, arithmetic and copies ran while one was open for 1% of the time, Pallas kernels for 0%

commit v1 on v0

v1 whole, which is shorter than its diff:
```python
import functools

import jax
import jax.numpy as jnp
from jax import lax
from jax.experimental import pallas as pl
from jax.experimental.pallas import tpu as pltpu
from jax.sharding import PartitionSpec as P

MESH = pl.DeviceIdType.MESH
PICK = 16
CHUNK = 256
LANES = 128


def kernel(
    sizes,
    ids_ref,
    emb_hbm,
    prior_ref,
    dist_ref,
    mean_ref,
    emb,
    wide,
    pick_wide,
    picks,
    parts,
    blocks,
    centers,
    half,
    norms,
    best,
    own_total,
    totals,
    load_sem,
    send_sem,
    part_sem,
    block_sem,
    center_sem,
    total_sem,
):
    groups, devs, rounds, seeds, rows, width = sizes
    me_grp = lax.axis_index("grp")
    me = lax.axis_index("dev")
    base = (me_grp * devs + me) * rows
    share = seeds // devs
    pieces = load_sem.shape[0]
    piece = rows // pieces
    slots = picks.shape[0]

    def load(k):
        return pltpu.make_async_copy(
            emb_hbm.at[pl.ds(k * piece, piece)], emb.at[pl.ds(k * piece, piece)], load_sem.at[k]
        )

    for k in range(pieces):
        load(k).start()

    barrier = pltpu.get_barrier_semaphore()

    @pl.loop(1, devs)
    def _(p):
        pl.semaphore_signal(barrier, inc=1, device_id={"dev": lax.rem(me + p, devs)}, device_id_type=MESH)

    for p in range(1, groups):
        pl.semaphore_signal(
            barrier, inc=1, device_id={"grp": lax.rem(me_grp + p, groups)}, device_id_type=MESH
        )

    wide[pl.ds(rows, 8), :] = jnp.zeros((8, width), jnp.float32)
    for k in range(pieces):
        load(k).wait()

        @pl.loop(0, piece // 128)
        def _(t, k=k):
            at = pl.multiple_of(k * piece + t * 128, 128)
            wide[pl.ds(at, 128), :] = emb[pl.ds(at, 128), :].astype(jnp.float32)

    def pick(slot):
        which = me_grp + groups * slot

        @pl.loop(0, seeds // PICK)
        def _(t):
            for u in range(PICK):
                at = ids_ref[which, t * PICK + u] - base
                inside = (at >= 0) & (at < rows)
                at = jnp.where(inside, at, rows)
                pick_wide[u, :, :] = wide[pl.ds(at, 1), :]
            picks[slot, t, :, :] = pick_wide[...].reshape(PICK, width).astype(jnp.bfloat16)

    def scatter(slot):
        @pl.loop(1, devs)
        def _(p):
            to = lax.rem(me + p, devs)
            pltpu.make_async_remote_copy(
                src_ref=picks.at[slot, to],
                dst_ref=parts.at[slot, me],
                send_sem=send_sem.at[slot],
                recv_sem=part_sem.at[slot],
                device_id={"dev": to},
                device_id_type=MESH,
            ).start()

        parts[slot, pl.ds(me, 1)] = picks[slot, pl.ds(me, 1)]

    def take(slot):
        peers = parts.at[slot, pl.ds(0, devs - 1)]
        pltpu.make_async_copy(peers, peers, part_sem.at[slot]).wait()
        total = jnp.sum(parts[slot].astype(jnp.float32), axis=0)
        blocks[me_grp + groups * slot] = total.astype(jnp.bfloat16)

    def trade(slot):
        index = me_grp + groups * slot
        for p in range(1, groups):
            pltpu.make_async_remote_copy(
                src_ref=blocks.at[index],
                dst_ref=blocks.at[index],
                send_sem=send_sem.at[2 + slot],
                recv_sem=block_sem.at[slot],
                device_id={"grp": lax.rem(me_grp + p, groups)},
                device_id_type=MESH,
            ).start()

    def arrived(ref, sem):
        pltpu.make_async_copy(ref, ref, sem).wait()

    def spread(r):
        @pl.loop(1, devs)
        def _(p):
            pltpu.make_async_remote_copy(
                src_ref=blocks.at[r],
                dst_ref=centers.at[r, me],
                send_sem=send_sem.at[4 + r],
                recv_sem=center_sem.at[r],
                device_id={"dev": lax.rem(me + p, devs)},
                device_id_type=MESH,
            ).start()

        centers[r, pl.ds(me, 1)] = blocks[pl.ds(r, 1)]

    tail = rounds - groups
    pick(0)
    pl.semaphore_wait(barrier, devs - 1 + groups - 1)
    scatter(0)

    @pl.when(me_grp < tail)
    def _():
        pick(1)
        scatter(1)

    ones = jnp.ones((16, width), jnp.bfloat16)

    @pl.loop(0, rows // CHUNK)
    def _(j):
        at = pl.multiple_of(j * CHUNK, CHUNK)
        x = wide[pl.ds(at, CHUNK), :]
        square = x * x
        high = square.astype(jnp.bfloat16)
        low = (square - high.astype(jnp.float32)).astype(jnp.bfloat16)
        over = (((1,), (1,)), ((), ()))
        total = lax.dot_general(ones, high, over, preferred_element_type=jnp.float32)
        total += lax.dot_general(ones, low, over, preferred_element_type=jnp.float32)
        for c in range(CHUNK // LANES):
            norms[pl.ds(j * (CHUNK // LANES) + c, 1), :] = total[0:1, c * LANES : (c + 1) * LANES]

    take(0)
    trade(0)
    arrived(blocks.at[pl.ds(0, groups - 1)], block_sem.at[0])
    for r in range(groups):
        spread(r)

    @pl.when(me_grp < tail)
    def _():
        take(1)
        trade(1)
        arrived(blocks.at[pl.ds(0, tail - 1)], block_sem.at[1])

    @pl.when(me_grp >= tail)
    def _():
        arrived(blocks.at[pl.ds(0, tail)], block_sem.at[1])

    for r in range(groups, rounds):
        spread(r)

    current = prior_ref[...]
    for r in range(rounds):
        arrived(centers.at[r, pl.ds(0, devs - 1)], center_sem.at[r])
        c = centers[r].reshape(seeds, width)
        wide_c = c.astype(jnp.float32)
        half[...] = jnp.broadcast_to(
            0.5 * jnp.sum(wide_c * wide_c, axis=1, keepdims=True), (seeds, LANES)
        )

        @pl.loop(0, rows // CHUNK)
        def _(j, r=r):
            at = pl.multiple_of(j * CHUNK, CHUNK)
            x = emb[pl.ds(at, CHUNK), :]
            c = centers[r].reshape(seeds, width)
            product = lax.dot_general(
                c, x, (((1,), (1,)), ((), ())), preferred_element_type=jnp.float32
            )
            for k in range(CHUNK // LANES):
                short = product[:, k * LANES : (k + 1) * LANES] - half[...]
                best[pl.ds(j * (CHUNK // LANES) + k, 1), :] = jnp.max(short, axis=0, keepdims=True)

        nearest = jnp.maximum(norms[...] - 2.0 * best[...], 0.0) / float(width)
        current = jnp.minimum(current, nearest)
        own_total[pl.ds(r, 1), :] = jnp.sum(current, axis=0, keepdims=True)

    dist_ref[...] = current
    own_total[pl.ds(rounds, 8 - rounds), :] = jnp.zeros((8 - rounds, LANES), jnp.float32)

    @pl.loop(1, devs)
    def _(p):
        pltpu.make_async_remote_copy(
            src_ref=own_total,
            dst_ref=totals.at[me],
            send_sem=send_sem.at[4 + rounds],
            recv_sem=total_sem,
            device_id={"dev": lax.rem(me + p, devs)},
            device_id_type=MESH,
        ).start()

    totals[pl.ds(me, 1)] = own_total[...][None]
    arrived(totals.at[pl.ds(0, devs - 1)], total_sem)
    group_sum = jnp.sum(jnp.sum(totals[...], axis=0), axis=1, keepdims=True)
    mean_ref[...] = jnp.broadcast_to(group_sum / float(rows * devs), (8, LANES))

    arrived(parts.at[0, pl.ds(0, devs - 1)], send_sem.at[0])
    arrived(blocks.at[pl.ds(0, groups - 1)], send_sem.at[2])

    @pl.when(me_grp < tail)
    def _():
        arrived(parts.at[1, pl.ds(0, devs - 1)], send_sem.at[1])
        arrived(blocks.at[pl.ds(0, groups - 1)], send_sem.at[3])

    for r in range(rounds):
        arrived(centers.at[r, pl.ds(0, devs - 1)], send_sem.at[4 + r])
    arrived(totals.at[pl.ds(0, devs - 1)], send_sem.at[4 + rounds])


def body(embeddings, prior_dist, seed_ids):
    rows, width = embeddings.shape
    rounds, seeds = seed_ids.shape
    groups, devs = lax.axis_size("grp"), lax.axis_size("dev")
    share = seeds // devs
    slots = -(-rounds // groups)
    sizes = (groups, devs, rounds, seeds, rows, width)
    vmem = pl.BlockSpec(memory_space=pltpu.VMEM)
    dist, means = pl.pallas_call(
        functools.partial(kernel, sizes),
        name="seeding",
        out_shape=(
            jax.ShapeDtypeStruct((rows // LANES, LANES), jnp.float32),
            jax.ShapeDtypeStruct((8, LANES), jnp.float32),
        ),
        in_specs=[
            pl.BlockSpec(memory_space=pltpu.SMEM),
            pl.BlockSpec(memory_space=pl.ANY),
            vmem,
        ],
        out_specs=(vmem, vmem),
        scratch_shapes=[
            pltpu.VMEM((rows, width), jnp.bfloat16),
            pltpu.VMEM((rows + 8, width), jnp.float32),
            pltpu.VMEM((PICK, 1, width), jnp.float32),
            pltpu.VMEM((slots, devs, share, width), jnp.bfloat16),
            pltpu.VMEM((slots, devs, share, width), jnp.bfloat16),
            pltpu.VMEM((rounds, share, width), jnp.bfloat16),
            pltpu.VMEM((rounds, devs, share, width), jnp.bfloat16),
            pltpu.VMEM((seeds, LANES), jnp.float32),
            pltpu.VMEM((rows // LANES, LANES), jnp.float32),
            pltpu.VMEM((rows // LANES, LANES), jnp.float32),
            pltpu.VMEM((8, LANES), jnp.float32),
            pltpu.VMEM((devs, 8, LANES), jnp.float32),
            pltpu.SemaphoreType.DMA((8,)),
            pltpu.SemaphoreType.DMA((5 + rounds,)),
            pltpu.SemaphoreType.DMA((2,)),
            pltpu.SemaphoreType.DMA((2,)),
            pltpu.SemaphoreType.DMA((rounds,)),
            pltpu.SemaphoreType.DMA,
        ],
        compiler_params=pltpu.CompilerParams(
            collective_id=0, has_side_effects=True, vmem_limit_bytes=56 * 1024 * 1024
        ),
    )(seed_ids, embeddings, prior_dist.reshape(rows // LANES, LANES))
    return dist.reshape(rows), means[:rounds, :1]


def solution(mesh):
    placed = (P(("grp", "dev"), None), P(("grp", "dev")), P())
    return jax.shard_map(
        body,
        mesh=mesh,
        in_specs=placed,
        out_specs=(P(("grp", "dev")), P(None, "grp")),
        check_vma=False,
    )
```

time: 276 us -> 94.4 us (0.34)
  waiting for transfers between devices: 159 us -> 0 us
  Pallas kernels: 0 us -> 90.8 us
  matrix products: 54.8 us -> 0 us
  local copies, waits for them, and re-layouts: 21.8 us -> 2.64 us
  blocking collectives: 14.6 us -> 0 us
  between operations: 14.2 us -> 0.64 us
  other arithmetic: 9.52 us -> 0 us
    psum x2 -> x0, waiting for transfers between devices: 159 us -> none  [the longest x1 110 us: body(): owned = lax.psum(picked.astype(jnp.bfloat16), 'dev')]
    pallas_call x0 -> x1, Pallas kernels: none -> 90.8 us  [body(): pl.pallas_call(functools.partial(kernel, sizes), name='seeding', out_shap...]
    dot_general x24 -> x0, matrix products: 54.8 us -> none  [block_gaps(): products = jnp.dot(block, centers.T, preferred_element_type=jnp.float32)]
    all_to_all x1 -> x0, blocking collectives: 14.6 us -> none  [from_everyone(): return lax.all_to_all(copies, axis, split_axis=0, concat_axis=0, tiled=True)]
    gather x1 -> x0, local copies, waits for them, and re-layouts: 12.5 us -> none  [body(): picked = jnp.take(embeddings, jnp.clip(offsets, 0, row_count - 1), axis=0)]
    reduce_sum x5 -> x0, other arithmetic: 5.88 us -> none  [the longest x1 3.34 us: body(): row_norms = jnp.sum(jnp.square(embeddings.astype(jnp.float32)), axis=1)]
    another operation x7 -> x0, local copies, waits for them, and re-layouts: 3.88 us -> none  [the longest x1 3.85 us: body(): summed_totals = of_everyone(jnp.stack(partial_value), 'dev')]
    dynamic_update_slice x24 -> x0, local copies, waits for them, and re-layouts: 3.12 us -> none  [body(): lax.map(one_round, (blocks, norm_blocks)).reshape(row_count)]
  transfers between devices with their start and end apart: 2 -> 0, of which waited for: 2 -> 0; matrix products, arithmetic and copies ran while one was open for 1% -> 0% of each run, Pallas kernels for 0% -> 0%
where the time goes in v1:
time: 94.4 us; the launch traced here: 94.1 us
  Pallas kernels  90.8 us (96%)
  local copies, waits for them, and re-layouts  2.64 us (3%)
    pallas_call x1, Pallas kernels, body(): pl.pallas_call(functools.partial(kernel, sizes), name='seeding', out_shap...  90.8 us
    unnamed x2, local copies, waits for them, and re-layouts  2.64 us

profile of v1, /device:TPU:1, one launch (start us, length us, event | category | flops | bytes accessed | tf_op | source)
XLA Modules:
  0.0 94.1 jit_solution(9791609389909161585)
XLA Ops:
  0.6 90.8 %seeding.1 = (f32[64,128]{1,0:T(8,128)}, f32[8,128]{1,0:T(8,128)}) custom-call(s32[6,512]{1,0:T(8,128)} %ids_ref.1, bf16[8192,256]{1,0:T(8,128)(2,1)} %emb_hbm.1, f32[64,128]{1,0:T(8,128)} %bitcast.3), custom_call_target="tpu_custom_call" | custom-call | tf_op jit(solution)/shard_map/seeding/pallas_call | solution.py:250
  91.4 1.3 %copy.5 = f32[6,1]{0,1:T(1,128)} copy(f32[6,1]{1,0:T(8,128)} %bitcast.5) | data formatting | bytes 48
  92.7 1.4 %copy.7 = f32[8192]{0:T(1024)} copy(f32[8192]{0:T(1024)} %bitcast.4) | data formatting | bytes 65536

commit v2 on v1

--- a/solution.py
+++ b/solution.py
@@ -11,9 +11,91 @@
 PICK = 16
 CHUNK = 256
 LANES = 128
-
-
-def kernel(
+PIECE = 128
+PIECES = 7
+NORM_ROWS = 16
+
+
+def tile_of(emb, j):
+    return emb[pl.ds(pl.multiple_of(j * CHUNK, CHUNK), CHUNK), :]
+
+
+def row_norms(emb, norms, accs):
+    width = emb.shape[1]
+    ones = jnp.ones((NORM_ROWS, width), jnp.bfloat16)
+    steps = 4
+
+    @pl.loop(0, emb.shape[0] // CHUNK // (2 * steps))
+    def _(t):
+        for i in range(steps):
+            for q in range(2):
+                j = (t * steps + i) * 2 + q
+                x = tile_of(emb, j).astype(jnp.float32)
+                square = x * x
+                high = square.astype(jnp.bfloat16)
+                low = (square - high.astype(jnp.float32)).astype(jnp.bfloat16)
+                acc = accs[q][PIECES + i]
+                for part in (high, low):
+                    pltpu.matmul_push_rhs(part, staging_register=0, mxu_index=q, transpose=True)
+                    pltpu.matmul_acc_lhs(acc, ones, load_staged_rhs=0)
+                total = pltpu.matmul_pop(acc)
+                for k in range(CHUNK // LANES):
+                    norms[pl.ds(j * (CHUNK // LANES) + k, 1), :] = total[
+                        0:1, k * LANES : (k + 1) * LANES
+                    ]
+
+
+def nearest_of(emb, center, half, best, accs):
+    devs, share, width = center.shape
+    seeds = devs * share
+    wide_c = center[...].reshape(seeds, width).astype(jnp.float32)
+    half[...] = jnp.broadcast_to(
+        0.5 * jnp.sum(wide_c * wide_c, axis=1, keepdims=True), (seeds, LANES)
+    )
+    trips = emb.shape[0] // CHUNK // 2
+    count = 0
+    for q in range(2):
+        pltpu.matmul_push_rhs(tile_of(emb, q), staging_register=0, mxu_index=q, transpose=True)
+    for t in range(trips):
+        run = {}
+        for p in range(seeds // PIECE):
+            lhs = center[pl.ds(p * PIECE // share, PIECE // share)].reshape(PIECE, width)
+            use = [accs[q][count % PIECES] for q in range(2)]
+            for q in range(2):
+                pltpu.matmul_acc_lhs(use[q], lhs, load_staged_rhs=0 if p == 0 else None)
+            if p == 0 and t + 1 < trips:
+                for q in range(2):
+                    pltpu.matmul_push_rhs(
+                        tile_of(emb, (t + 1) * 2 + q), staging_register=0, mxu_index=q, transpose=True
+                    )
+            offset = half[pl.ds(p * PIECE, PIECE), :]
+            for q in range(2):
+                value = pltpu.matmul_pop(use[q])
+                for k in range(CHUNK // LANES):
+                    short = value[:, k * LANES : (k + 1) * LANES] - offset
+                    short = jnp.max(short.reshape(PIECE // 8, 8, LANES), axis=0)
+                    run[q, k] = jnp.maximum(run[q, k], short) if p else short
+            count += 1
+        for (q, k), value in run.items():
+            row = (t * 2 + q) * (CHUNK // LANES) + k
+            best[pl.ds(row, 1), :] = jnp.max(value, axis=0, keepdims=True)
+
+
+def kernel(sizes, *refs):
+    specs = [
+        pltpu.ACC(q)((rows, CHUNK), jnp.float32)
+        for q in range(2)
+        for rows in [PIECE] * PIECES + [NORM_ROWS] * 4
+    ]
+
+    def inner(*accs):
+        half = len(accs) // 2
+        run_kernel(sizes, *refs, (accs[:half], accs[half:]))
+
+    pl.run_scoped(inner, *specs)
+
+
+def run_kernel(
     sizes,
     ids_ref,
     emb_hbm,
@@ -38,6 +120,7 @@
     block_sem,
     center_sem,
     total_sem,
+    accs,
 ):
     groups, devs, rounds, seeds, rows, width = sizes
     me_grp = lax.axis_index("grp")
@@ -148,20 +231,7 @@
         pick(1)
         scatter(1)
 
-    ones = jnp.ones((16, width), jnp.bfloat16)
-
-    @pl.loop(0, rows // CHUNK)
-    def _(j):
-        at = pl.multiple_of(j * CHUNK, CHUNK)
-        x = wide[pl.ds(at, CHUNK), :]
-        square = x * x
-        high = square.astype(jnp.bfloat16)
-        low = (square - high.astype(jnp.float32)).astype(jnp.bfloat16)
-        over = (((1,), (1,)), ((), ()))
-        total = lax.dot_general(ones, high, over, preferred_element_type=jnp.float32)
-        total += lax.dot_general(ones, low, over, preferred_element_type=jnp.float32)
-        for c in range(CHUNK // LANES):
-            norms[pl.ds(j * (CHUNK // LANES) + c, 1), :] = total[0:1, c * LANES : (c + 1) * LANES]
+    row_norms(emb, norms, accs)
 
     take(0)
     trade(0)
@@ -182,33 +252,16 @@
     for r in range(groups, rounds):
         spread(r)
 
-    current = prior_ref[...]
-    for r in range(rounds):
+    dist_ref[...] = prior_ref[...]
+    own_total[...] = jnp.zeros((8, LANES), jnp.float32)
+    @pl.loop(0, rounds)
+    def _(r):
         arrived(centers.at[r, pl.ds(0, devs - 1)], center_sem.at[r])
-        c = centers[r].reshape(seeds, width)
-        wide_c = c.astype(jnp.float32)
-        half[...] = jnp.broadcast_to(
-            0.5 * jnp.sum(wide_c * wide_c, axis=1, keepdims=True), (seeds, LANES)
-        )
-
-        @pl.loop(0, rows // CHUNK)
-        def _(j, r=r):
-            at = pl.multiple_of(j * CHUNK, CHUNK)
-            x = emb[pl.ds(at, CHUNK), :]
-            c = centers[r].reshape(seeds, width)
-            product = lax.dot_general(
-                c, x, (((1,), (1,)), ((), ())), preferred_element_type=jnp.float32
-            )
-            for k in range(CHUNK // LANES):
-                short = product[:, k * LANES : (k + 1) * LANES] - half[...]
-                best[pl.ds(j * (CHUNK // LANES) + k, 1), :] = jnp.max(short, axis=0, keepdims=True)
-
+        nearest_of(emb, centers.at[r], half, best, accs)
         nearest = jnp.maximum(norms[...] - 2.0 * best[...], 0.0) / float(width)
-        current = jnp.minimum(current, nearest)
+        current = jnp.minimum(dist_ref[...], nearest)
+        dist_ref[...] = current
         own_total[pl.ds(r, 1), :] = jnp.sum(current, axis=0, keepdims=True)
-
-    dist_ref[...] = current
-    own_total[pl.ds(rounds, 8 - rounds), :] = jnp.zeros((8 - rounds, LANES), jnp.float32)
 
     @pl.loop(1, devs)
     def _(p):

time: 94.4 us -> 54.4 us (0.58)
  Pallas kernels: 90.8 us -> 50.8 us
    pallas_call x1, Pallas kernels: 90.8 us -> 50.8 us  [body(): pl.pallas_call(functools.partial(kernel, sizes), name='seeding', out_shap...]
where the time goes in v2:
time: 54.4 us; the launch traced here: 54.1 us
  Pallas kernels  50.8 us (93%)
  local copies, waits for them, and re-layouts  2.64 us (5%)
  between operations  0.64 us (1%)
    pallas_call x1, Pallas kernels, body(): pl.pallas_call(functools.partial(kernel, sizes), name='seeding', out_shap...  50.8 us
    unnamed x2, local copies, waits for them, and re-layouts  2.64 us

profile of v2, /device:TPU:1, one launch (start us, length us, event | category | flops | bytes accessed | tf_op | source)
XLA Modules:
  0.0 54.1 jit_solution(12620936294479350937)
XLA Ops:
  0.6 50.8 %seeding.1 = (f32[64,128]{1,0:T(8,128)}, f32[8,128]{1,0:T(8,128)}) custom-call(s32[6,512]{1,0:T(8,128)} %refs_0_.1, bf16[8192,256]{1,0:T(8,128)(2,1)} %refs_1_.1, f32[64,128]{1,0:T(8,128)} %bitcast.3), custom_call_target="tpu_custom_call" | custom-call | tf_op jit(solution)/shard_map/seeding/pallas_call | solution.py:303
  51.4 1.3 %copy.5 = f32[6,1]{0,1:T(1,128)} copy(f32[6,1]{1,0:T(8,128)} %bitcast.5) | data formatting | bytes 48
  52.7 1.4 %copy.7 = f32[8192]{0:T(1024)} copy(f32[8192]{0:T(1024)} %bitcast.4) | data formatting | bytes 65536

commit v3 on v2

--- a/solution.py
+++ b/solution.py
@@ -8,7 +8,7 @@
 from jax.sharding import PartitionSpec as P
 
 MESH = pl.DeviceIdType.MESH
-PICK = 16
+PICK = 32
 CHUNK = 256
 LANES = 128
 PIECE = 128
@@ -45,9 +45,10 @@
                     ]
 
 
-def nearest_of(emb, center, half, best, accs):
-    devs, share, width = center.shape
-    seeds = devs * share
+def nearest_of(emb, center, half, best, accs, middle):
+    cores, chips, share, width = center.shape
+    seeds = cores * chips * share
+    side = chips * share
     wide_c = center[...].reshape(seeds, width).astype(jnp.float32)
     half[...] = jnp.broadcast_to(
         0.5 * jnp.sum(wide_c * wide_c, axis=1, keepdims=True), (seeds, LANES)
@@ -57,9 +58,12 @@
     for q in range(2):
         pltpu.matmul_push_rhs(tile_of(emb, q), staging_register=0, mxu_index=q, transpose=True)
     for t in range(trips):
+        if t == trips // 2:
+            middle()
         run = {}
         for p in range(seeds // PIECE):
-            lhs = center[pl.ds(p * PIECE // share, PIECE // share)].reshape(PIECE, width)
+            at = p * PIECE % side // share
+            lhs = center[p * PIECE // side, pl.ds(at, PIECE // share)].reshape(PIECE, width)
             use = [accs[q][count % PIECES] for q in range(2)]
             for q in range(2):
                 pltpu.matmul_acc_lhs(use[q], lhs, load_staged_rhs=0 if p == 0 else None)
@@ -95,14 +99,20 @@
     pl.run_scoped(inner, *specs)
 
 
+def arrived(ref, sem):
+    pltpu.make_async_copy(ref, ref, sem).wait()
+
+
 def run_kernel(
     sizes,
-    ids_ref,
+    ids_hbm,
     emb_hbm,
-    prior_ref,
+    prior_hbm,
     dist_ref,
     mean_ref,
+    ids,
     emb,
+    prior,
     wide,
     pick_wide,
     picks,
@@ -112,32 +122,53 @@
     half,
     norms,
     best,
+    nearest,
+    own_rows,
     own_total,
     totals,
     load_sem,
+    id_sem,
+    prior_sem,
     send_sem,
     part_sem,
     block_sem,
     center_sem,
+    relay_sem,
     total_sem,
     accs,
 ):
     groups, devs, rounds, seeds, rows, width = sizes
     me_grp = lax.axis_index("grp")
     me = lax.axis_index("dev")
+    cores = 2
+    chips = devs // cores
+    chip, core = me // cores, lax.rem(me, cores)
     base = (me_grp * devs + me) * rows
     share = seeds // devs
     pieces = load_sem.shape[0]
     piece = rows // pieces
-    slots = picks.shape[0]
+    tail = rounds - groups
 
     def load(k):
         return pltpu.make_async_copy(
             emb_hbm.at[pl.ds(k * piece, piece)], emb.at[pl.ds(k * piece, piece)], load_sem.at[k]
         )
 
+    def load_ids(slot):
+        which = me_grp + groups * slot
+        return pltpu.make_async_copy(
+            ids_hbm.at[pl.ds(which, 1)], ids.at[pl.ds(slot, 1)], id_sem.at[slot]
+        )
+
+    load_ids(0).start()
     for k in range(pieces):
         load(k).start()
+    load_prior = pltpu.make_async_copy(prior_hbm, prior, prior_sem)
+    load_prior.start()
+
+    @pl.when(me_grp < tail)
+    def _():
+        load_ids(1).start()
 
     barrier = pltpu.get_barrier_semaphore()
 
@@ -150,26 +181,34 @@
             barrier, inc=1, device_id={"grp": lax.rem(me_grp + p, groups)}, device_id_type=MESH
         )
 
-    wide[pl.ds(rows, 8), :] = jnp.zeros((8, width), jnp.float32)
+    wide[pl.ds(2 * rows, 16), :] = jnp.zeros((16, LANES), jnp.float32)
     for k in range(pieces):
         load(k).wait()
 
         @pl.loop(0, piece // 128)
         def _(t, k=k):
             at = pl.multiple_of(k * piece + t * 128, 128)
-            wide[pl.ds(at, 128), :] = emb[pl.ds(at, 128), :].astype(jnp.float32)
+            x = emb[pl.ds(at, 128), :].astype(jnp.float32)
+            for h in range(2):
+                wide[pl.ds(2 * at + h, 128, stride=2), :] = x[:, h * LANES : (h + 1) * LANES]
 
     def pick(slot):
-        which = me_grp + groups * slot
+        load_ids(slot).wait()
 
         @pl.loop(0, seeds // PICK)
         def _(t):
             for u in range(PICK):
-                at = ids_ref[which, t * PICK + u] - base
+                at = ids[slot, t * PICK + u] - base
                 inside = (at >= 0) & (at < rows)
-                at = jnp.where(inside, at, rows)
-                pick_wide[u, :, :] = wide[pl.ds(at, 1), :]
-            picks[slot, t, :, :] = pick_wide[...].reshape(PICK, width).astype(jnp.bfloat16)
+                at = jnp.where(inside, 2 * at, 2 * rows)
+                pick_wide[pl.ds(2 * (t * PICK + u), 2), :] = wide[pl.ds(at, 2), :]
+
+        @pl.loop(0, devs, unroll=4)
+        def _(t):
+            for h in range(2):
+                picks[slot, t, :, h * LANES : (h + 1) * LANES] = pick_wide[
+                    pl.ds(2 * share * t + h, share, stride=2), :
+                ].astype(jnp.bfloat16)
 
     def scatter(slot):
         @pl.loop(1, devs)
@@ -187,8 +226,7 @@
         parts[slot, pl.ds(me, 1)] = picks[slot, pl.ds(me, 1)]
 
     def take(slot):
-        peers = parts.at[slot, pl.ds(0, devs - 1)]
-        pltpu.make_async_copy(peers, peers, part_sem.at[slot]).wait()
+        arrived(parts.at[slot, pl.ds(0, devs - 1)], part_sem.at[slot])
         total = jnp.sum(parts[slot].astype(jnp.float32), axis=0)
         blocks[me_grp + groups * slot] = total.astype(jnp.bfloat16)
 
@@ -204,71 +242,106 @@
                 device_id_type=MESH,
             ).start()
 
-    def arrived(ref, sem):
-        pltpu.make_async_copy(ref, ref, sem).wait()
-
     def spread(r):
-        @pl.loop(1, devs)
+        @pl.loop(1, chips)
         def _(p):
             pltpu.make_async_remote_copy(
                 src_ref=blocks.at[r],
-                dst_ref=centers.at[r, me],
+                dst_ref=centers.at[r, core, chip],
                 send_sem=send_sem.at[4 + r],
                 recv_sem=center_sem.at[r],
-                device_id={"dev": lax.rem(me + p, devs)},
+                device_id={"dev": lax.rem(chip + p, chips) * cores + core},
                 device_id_type=MESH,
             ).start()
 
-        centers[r, pl.ds(me, 1)] = blocks[pl.ds(r, 1)]
-
-    tail = rounds - groups
+        centers[r, core, chip] = blocks[r]
+
+    def relay(r):
+        arrived(centers.at[r, 0, pl.ds(0, chips - 1)], center_sem.at[r])
+        pltpu.make_async_remote_copy(
+            src_ref=centers.at[r, core],
+            dst_ref=centers.at[r, core],
+            send_sem=send_sem.at[4 + rounds + r],
+            recv_sem=relay_sem.at[r],
+            device_id={"dev": chip * cores + 1 - core},
+            device_id_type=MESH,
+        ).start()
+
+    def turn(i):
+        lap = i // groups
+        return lap * groups + lax.rem(me_grp * (1 - lap) + i, groups)
+
     pick(0)
     pl.semaphore_wait(barrier, devs - 1 + groups - 1)
     scatter(0)
+    row_norms(emb, norms, accs)
 
     @pl.when(me_grp < tail)
     def _():
         pick(1)
-        scatter(1)
-
-    row_norms(emb, norms, accs)
 
     take(0)
+    spread(me_grp)
     trade(0)
-    arrived(blocks.at[pl.ds(0, groups - 1)], block_sem.at[0])
-    for r in range(groups):
-        spread(r)
 
     @pl.when(me_grp < tail)
     def _():
-        take(1)
-        trade(1)
-        arrived(blocks.at[pl.ds(0, tail - 1)], block_sem.at[1])
-
-    @pl.when(me_grp >= tail)
-    def _():
-        arrived(blocks.at[pl.ds(0, tail)], block_sem.at[1])
-
-    for r in range(groups, rounds):
-        spread(r)
-
-    dist_ref[...] = prior_ref[...]
-    own_total[...] = jnp.zeros((8, LANES), jnp.float32)
+        scatter(1)
+
+    arrived(blocks.at[pl.ds(0, groups - 1)], block_sem.at[0])
+    for i in range(1, groups):
+        spread(turn(i))
+    relay(me_grp)
+
     @pl.loop(0, rounds)
-    def _(r):
-        arrived(centers.at[r, pl.ds(0, devs - 1)], center_sem.at[r])
-        nearest_of(emb, centers.at[r], half, best, accs)
-        nearest = jnp.maximum(norms[...] - 2.0 * best[...], 0.0) / float(width)
-        current = jnp.minimum(dist_ref[...], nearest)
-        dist_ref[...] = current
-        own_total[pl.ds(r, 1), :] = jnp.sum(current, axis=0, keepdims=True)
+    def _(i):
+        r = turn(i)
+        arrived(centers.at[r, 0], relay_sem.at[r])
+
+        def middle():
+            @pl.when(i + 1 < rounds)
+            def _():
+                relay(turn(i + 1))
+
+            @pl.when((i == 0) & (me_grp < tail))
+            def _():
+                take(1)
+                trade(1)
+
+            @pl.when(i == 1)
+            def _():
+                @pl.when(me_grp < tail)
+                def _():
+                    arrived(blocks.at[pl.ds(0, tail - 1)], block_sem.at[1])
+
+                @pl.when(me_grp >= tail)
+                def _():
+                    arrived(blocks.at[pl.ds(0, tail)], block_sem.at[1])
+
+                for s in range(groups, rounds):
+                    spread(s)
+
+        nearest_of(emb, centers.at[r], half, best, accs, middle)
+        nearest[r] = jnp.maximum(norms[...] - 2.0 * best[...], 0.0) / float(width)
+
+    load_prior.wait()
+    current = prior[...]
+    own_rows[...] = jnp.zeros((8, LANES), jnp.float32)
+    for r in range(rounds):
+        current = jnp.minimum(current, nearest[r])
+        own_rows[pl.ds(r, 1), :] = jnp.sum(current, axis=0, keepdims=True)
+    dist_ref[...] = current
+    sums = jnp.broadcast_to(jnp.sum(own_rows[...], axis=1, keepdims=True), (8, LANES))
+    lane = lax.broadcasted_iota(jnp.int32, (8, LANES), 1)
+    row = lax.broadcasted_iota(jnp.int32, (8, LANES), 0)
+    own_total[...] = jnp.sum(jnp.where(lane == row, sums, 0.0), axis=0, keepdims=True)
 
     @pl.loop(1, devs)
     def _(p):
         pltpu.make_async_remote_copy(
             src_ref=own_total,
             dst_ref=totals.at[me],
-            send_sem=send_sem.at[4 + rounds],
+            send_sem=send_sem.at[4 + 2 * rounds],
             recv_sem=total_sem,
             device_id={"dev": lax.rem(me + p, devs)},
             device_id_type=MESH,
@@ -276,8 +349,7 @@
 
     totals[pl.ds(me, 1)] = own_total[...][None]
     arrived(totals.at[pl.ds(0, devs - 1)], total_sem)
-    group_sum = jnp.sum(jnp.sum(totals[...], axis=0), axis=1, keepdims=True)
-    mean_ref[...] = jnp.broadcast_to(group_sum / float(rows * devs), (8, LANES))
+    mean_ref[...] = jnp.sum(totals[...], axis=0) / float(rows * devs)
 
     arrived(parts.at[0, pl.ds(0, devs - 1)], send_sem.at[0])
     arrived(blocks.at[pl.ds(0, groups - 1)], send_sem.at[2])
@@ -288,8 +360,14 @@
         arrived(blocks.at[pl.ds(0, groups - 1)], send_sem.at[3])
 
     for r in range(rounds):
-        arrived(centers.at[r, pl.ds(0, devs - 1)], send_sem.at[4 + r])
-    arrived(totals.at[pl.ds(0, devs - 1)], send_sem.at[4 + rounds])
+        arrived(centers.at[r, 0, pl.ds(0, chips - 1)], send_sem.at[4 + r])
+        arrived(centers.at[r, 0], send_sem.at[4 + rounds + r])
+    arrived(totals.at[pl.ds(0, devs - 1)], send_sem.at[4 + 2 * rounds])
+
+
+def finish(dist_in, mean_in, dist_ref, mean_ref):
+    dist_ref[...] = dist_in[...]
+    mean_ref[...] = mean_in[:, : mean_ref.shape[1]]
 
 
 def body(embeddings, prior_dist, seed_ids):
@@ -299,45 +377,61 @@
     share = seeds // devs
     slots = -(-rounds // groups)
     sizes = (groups, devs, rounds, seeds, rows, width)
+    flat = (rows // LANES, LANES)
     vmem = pl.BlockSpec(memory_space=pltpu.VMEM)
+    hbm = pl.BlockSpec(memory_space=pltpu.HBM)
     dist, means = pl.pallas_call(
         functools.partial(kernel, sizes),
         name="seeding",
         out_shape=(
-            jax.ShapeDtypeStruct((rows // LANES, LANES), jnp.float32),
-            jax.ShapeDtypeStruct((8, LANES), jnp.float32),
+            jax.ShapeDtypeStruct(flat, jnp.float32),
+            jax.ShapeDtypeStruct((1, LANES), jnp.float32),
         ),
-        in_specs=[
-            pl.BlockSpec(memory_space=pltpu.SMEM),
-            pl.BlockSpec(memory_space=pl.ANY),
-            vmem,
-        ],
+        in_specs=[hbm, hbm, hbm],
         out_specs=(vmem, vmem),
         scratch_shapes=[
+            pltpu.SMEM((slots, seeds), jnp.int32),
             pltpu.VMEM((rows, width), jnp.bfloat16),
-            pltpu.VMEM((rows + 8, width), jnp.float32),
-            pltpu.VMEM((PICK, 1, width), jnp.float32),
+            pltpu.VMEM(flat, jnp.float32),
+            pltpu.VMEM((2 * rows + 16, LANES), jnp.float32),
+            pltpu.VMEM((2 * seeds, LANES), jnp.float32),
             pltpu.VMEM((slots, devs, share, width), jnp.bfloat16),
             pltpu.VMEM((slots, devs, share, width), jnp.bfloat16),
             pltpu.VMEM((rounds, share, width), jnp.bfloat16),
-            pltpu.VMEM((rounds, devs, share, width), jnp.bfloat16),
+            pltpu.VMEM((rounds, 2, devs // 2, share, width), jnp.bfloat16),
             pltpu.VMEM((seeds, LANES), jnp.float32),
-            pltpu.VMEM((rows // LANES, LANES), jnp.float32),
-            pltpu.VMEM((rows // LANES, LANES), jnp.float32),
+            pltpu.VMEM(flat, jnp.float32),
+            pltpu.VMEM(flat, jnp.float32),
+            pltpu.VMEM((rounds, *flat), jnp.float32),
             pltpu.VMEM((8, LANES), jnp.float32),
-            pltpu.VMEM((devs, 8, LANES), jnp.float32),
+            pltpu.VMEM((1, LANES), jnp.float32),
+            pltpu.VMEM((devs, 1, LANES), jnp.float32),
             pltpu.SemaphoreType.DMA((8,)),
-            pltpu.SemaphoreType.DMA((5 + rounds,)),
+            pltpu.SemaphoreType.DMA((slots,)),
+            pltpu.SemaphoreType.DMA,
+            pltpu.SemaphoreType.DMA((5 + 2 * rounds,)),
             pltpu.SemaphoreType.DMA((2,)),
             pltpu.SemaphoreType.DMA((2,)),
+            pltpu.SemaphoreType.DMA((rounds,)),
             pltpu.SemaphoreType.DMA((rounds,)),
             pltpu.SemaphoreType.DMA,
         ],
         compiler_params=pltpu.CompilerParams(
-            collective_id=0, has_side_effects=True, vmem_limit_bytes=56 * 1024 * 1024
+            collective_id=0, has_side_effects=True, vmem_limit_bytes=67_000_000
         ),
-    )(seed_ids, embeddings, prior_dist.reshape(rows // LANES, LANES))
-    return dist.reshape(rows), means[:rounds, :1]
+    )(seed_ids, embeddings, prior_dist.reshape(flat))
+    dist, means = pl.pallas_call(
+        finish,
+        name="finish",
+        out_shape=(
+            jax.ShapeDtypeStruct(flat, jnp.float32),
+            jax.ShapeDtypeStruct((1, rounds), jnp.float32),
+        ),
+        in_specs=[vmem, vmem],
+        out_specs=(vmem, vmem),
+        compiler_params=pltpu.CompilerParams(vmem_limit_bytes=1024 * 1024),
+    )(dist, means)
+    return dist.reshape(rows), means.reshape(rounds, 1)
 
 
 def solution(mesh):

time: 54.4 us -> 48.4 us (0.89)
  Pallas kernels: 50.8 us -> 46.2 us
  local copies, waits for them, and re-layouts: 2.64 us -> 1.35 us
    pallas_call x1, Pallas kernels: 50.8 us -> 45.6 us  [body(): pl.pallas_call(functools.partial(kernel, sizes), name='seeding', out_shap...]
    unnamed x2 -> x4, local copies, waits for them, and re-layouts: 2.64 us -> 1.35 us
    pallas_call x0 -> x1, Pallas kernels: none -> 0.62 us  [body(): pl.pallas_call(finish, name='finish', out_shape=(jax.ShapeDtypeStruct(fla...]
where the time goes in v3:
time: 48.4 us; the launch traced here: 48.2 us
  Pallas kernels  46.2 us (95%)
  local copies, waits for them, and re-layouts  1.35 us (3%)
  between operations  0.65 us (1%)
    pallas_call x1, Pallas kernels, body(): pl.pallas_call(functools.partial(kernel, sizes), name='seeding', out_shap...  45.6 us
    unnamed x4, local copies, waits for them, and re-layouts  1.35 us

profile of v3, /device:TPU:1, one launch (start us, length us, event | category | flops | bytes accessed | tf_op | source)
XLA Modules:
  0.0 48.2 jit_solution(9502977026306070100)
XLA Ops:
  0.6 45.6 %seeding.1 = (f32[64,128]{1,0:T(8,128)}, f32[1,128]{1,0:T(1,128)}) custom-call(s32[6,512]{1,0:T(8,128)} %refs_0_.1, bf16[8192,256]{1,0:T(8,128)(2,1)} %refs_1_.1, f32[64,128]{1,0:T(8,128)} %bitcast.3), custom_call_target="tpu_custom_call" | custom-call | tf_op jit(solution)/shard_map/seeding/pallas_call | solution.py:383
  46.2 0.0 copy-start
  46.2 0.7 %copy-done = f32[64,128]{1,0:T(8,128)S(1)} copy-done((f32[64,128]{1,0:T(8,128)S(1)}, f32[64,128]{1,0:T(8,128)}, u32[]{:S(2)}) %copy-start) | copy-done | bytes 32792
  47.0 0.0 copy-start.1
  47.0 0.6 %copy-done.1 = f32[1,128]{1,0:T(1,128)S(1)} copy-done((f32[1,128]{1,0:T(1,128)S(1)}, f32[1,128]{1,0:T(1,128)}, u32[]{:S(2)}) %copy-start.1) | copy-done | bytes 536
  47.6 0.6 %finish.1 = (f32[64,128]{1,0:T(8,128)}, f32[1,6]{1,0:T(1,128)}) custom-call(f32[64,128]{1,0:T(8,128)S(1)} %copy-done, f32[1,128]{1,0:T(1,128)S(1)} %copy-done.1), custom_call_target="tpu_custom_call" | custom-call | tf_op jit(solution)/shard_map/finish/pallas_call | solution.py:423
Async XLA Ops:
  46.2 0.8 %copy-start = (f32[64,128]{1,0:T(8,128)S(1)}, f32[64,128]{1,0:T(8,128)}, u32[]{:S(2)}) copy-start(f32[64,128]{1,0:T(8,128)} %get-tuple-element.6.dist_in) | copy-start | bytes 98308
  47.0 0.6 %copy-start.1 = (f32[1,128]{1,0:T(1,128)S(1)}, f32[1,128]{1,0:T(1,128)}, u32[]{:S(2)}) copy-start(f32[1,128]{1,0:T(1,128)} %get-tuple-element.7.mean_in) | copy-start | bytes 1540

commit v4 on v3

--- a/solution.py
+++ b/solution.py
@@ -13,6 +13,8 @@
 LANES = 128
 PIECE = 128
 PIECES = 7
+LAG = 4
+EDGE = 8
 NORM_ROWS = 16
 
 
@@ -45,44 +47,64 @@
                     ]
 
 
-def nearest_of(emb, center, half, best, accs, middle):
-    cores, chips, share, width = center.shape
-    seeds = cores * chips * share
-    side = chips * share
-    wide_c = center[...].reshape(seeds, width).astype(jnp.float32)
-    half[...] = jnp.broadcast_to(
-        0.5 * jnp.sum(wide_c * wide_c, axis=1, keepdims=True), (seeds, LANES)
+def push_tiles(emb, t):
+    for q in range(2):
+        pltpu.matmul_push_rhs(
+            tile_of(emb, t * 2 + q), staging_register=0, mxu_index=q, transpose=True
+        )
+
+
+def half_norms(center, half, unit):
+    chips, share, width = center.shape
+    wide_c = center[...].reshape(chips * share, width).astype(jnp.float32)
+    half[unit] = jnp.broadcast_to(
+        0.5 * jnp.sum(wide_c * wide_c, axis=1, keepdims=True), (chips * share, LANES)
     )
+
+
+def nearest_of(emb, sides, half, best, accs, between):
+    chips, share, width = sides[0].shape
     trips = emb.shape[0] // CHUNK // 2
+    pieces = chips * share // PIECE
+    pending = []
+    run = {}
+
+    def pop():
+        unit, t, p, use = pending.pop(0)
+        offset = half[unit, pl.ds(p * PIECE, PIECE), :]
+        for q in range(2):
+            value = pltpu.matmul_pop(use[q])
+            for k in range(CHUNK // LANES):
+                short = value[:, k * LANES : (k + 1) * LANES] - offset
+                short = jnp.max(short.reshape(PIECE // 8, 8, LANES), axis=0)
+                run[q, k] = jnp.maximum(run[q, k], short) if p else short
+        if p == pieces - 1:
+            for (q, k), value in list(run.items()):
+                row = (t * 2 + q) * (CHUNK // LANES) + k
+                value = jnp.max(value, axis=0, keepdims=True)
+                if unit:
+                    value = jnp.maximum(value, best[pl.ds(row, 1), :])
+                best[pl.ds(row, 1), :] = value
+
     count = 0
-    for q in range(2):
-        pltpu.matmul_push_rhs(tile_of(emb, q), staging_register=0, mxu_index=q, transpose=True)
-    for t in range(trips):
-        if t == trips // 2:
-            middle()
-        run = {}
-        for p in range(seeds // PIECE):
-            at = p * PIECE % side // share
-            lhs = center[p * PIECE // side, pl.ds(at, PIECE // share)].reshape(PIECE, width)
-            use = [accs[q][count % PIECES] for q in range(2)]
-            for q in range(2):
-                pltpu.matmul_acc_lhs(use[q], lhs, load_staged_rhs=0 if p == 0 else None)
-            if p == 0 and t + 1 < trips:
+    for unit in range(2):
+        if unit:
+            between()
+        half_norms(sides[unit], half, unit)
+        for t in range(trips):
+            for p in range(pieces):
+                lhs = sides[unit][pl.ds(p * PIECE // share, PIECE // share)].reshape(PIECE, width)
+                use = [accs[q][count % PIECES] for q in range(2)]
+                count += 1
                 for q in range(2):
-                    pltpu.matmul_push_rhs(
-                        tile_of(emb, (t + 1) * 2 + q), staging_register=0, mxu_index=q, transpose=True
-                    )
-            offset = half[pl.ds(p * PIECE, PIECE), :]
-            for q in range(2):
-                value = pltpu.matmul_pop(use[q])
-                for k in range(CHUNK // LANES):
-                    short = value[:, k * LANES : (k + 1) * LANES] - offset
-                    short = jnp.max(short.reshape(PIECE // 8, 8, LANES), axis=0)
-                    run[q, k] = jnp.maximum(run[q, k], short) if p else short
-            count += 1
-        for (q, k), value in run.items():
-            row = (t * 2 + q) * (CHUNK // LANES) + k
-            best[pl.ds(row, 1), :] = jnp.max(value, axis=0, keepdims=True)
+                    pltpu.matmul_acc_lhs(use[q], lhs, load_staged_rhs=None if p else 0)
+                if p == 0:
+                    push_tiles(emb, (t + 1) % trips)
+                pending.append((unit, t, p, use))
+                if len(pending) > LAG:
+                    pop()
+    while pending:
+        pop()
 
 
 def kernel(sizes, *refs):
@@ -108,8 +130,7 @@
     ids_hbm,
     emb_hbm,
     prior_hbm,
-    dist_ref,
-    mean_ref,
+    both_ref,
     ids,
     emb,
     prior,
@@ -181,7 +202,8 @@
             barrier, inc=1, device_id={"grp": lax.rem(me_grp + p, groups)}, device_id_type=MESH
         )
 
-    wide[pl.ds(2 * rows, 16), :] = jnp.zeros((16, LANES), jnp.float32)
+    for edge in (0, EDGE + 2 * rows):
+        wide[pl.ds(edge, EDGE), :] = jnp.zeros((EDGE, LANES), jnp.float32)
     for k in range(pieces):
         load(k).wait()
 
@@ -190,7 +212,7 @@
             at = pl.multiple_of(k * piece + t * 128, 128)
             x = emb[pl.ds(at, 128), :].astype(jnp.float32)
             for h in range(2):
-                wide[pl.ds(2 * at + h, 128, stride=2), :] = x[:, h * LANES : (h + 1) * LANES]
+                wide[pl.ds(EDGE + 2 * at + h, 128, stride=2), :] = x[:, h * LANES : (h + 1) * LANES]
 
     def pick(slot):
         load_ids(slot).wait()
@@ -198,10 +220,8 @@
         @pl.loop(0, seeds // PICK)
         def _(t):
             for u in range(PICK):
-                at = ids[slot, t * PICK + u] - base
-                inside = (at >= 0) & (at < rows)
-                at = jnp.where(inside, 2 * at, 2 * rows)
-                pick_wide[pl.ds(2 * (t * PICK + u), 2), :] = wide[pl.ds(at, 2), :]
+                at = jnp.clip(ids[slot, t * PICK + u] - base, -1, rows)
+                pick_wide[pl.ds(2 * (t * PICK + u), 2), :] = wide[pl.ds(2 * at + EDGE, 2), :]
 
         @pl.loop(0, devs, unroll=4)
         def _(t):
@@ -281,8 +301,8 @@
         pick(1)
 
     take(0)
+    trade(0)
     spread(me_grp)
-    trade(0)
 
     @pl.when(me_grp < tail)
     def _():
@@ -291,38 +311,42 @@
     arrived(blocks.at[pl.ds(0, groups - 1)], block_sem.at[0])
     for i in range(1, groups):
         spread(turn(i))
-    relay(me_grp)
+    push_tiles(emb, 0)
 
     @pl.loop(0, rounds)
     def _(i):
         r = turn(i)
-        arrived(centers.at[r, 0], relay_sem.at[r])
-
-        def middle():
-            @pl.when(i + 1 < rounds)
+        relay(r)
+
+        @pl.when((i == 1) & (me_grp < tail))
+        def _():
+            take(1)
+            trade(1)
+
+        @pl.when(i == 2)
+        def _():
+            @pl.when(me_grp < tail)
             def _():
-                relay(turn(i + 1))
-
-            @pl.when((i == 0) & (me_grp < tail))
+                arrived(blocks.at[pl.ds(0, tail - 1)], block_sem.at[1])
+
+            @pl.when(me_grp >= tail)
             def _():
-                take(1)
-                trade(1)
-
-            @pl.when(i == 1)
-            def _():
-                @pl.when(me_grp < tail)
-                def _():
-                    arrived(blocks.at[pl.ds(0, tail - 1)], block_sem.at[1])
-
-                @pl.when(me_grp >= tail)
-                def _():
-                    arrived(blocks.at[pl.ds(0, tail)], block_sem.at[1])
-
-                for s in range(groups, rounds):
-                    spread(s)
-
-        nearest_of(emb, centers.at[r], half, best, accs, middle)
+                arrived(blocks.at[pl.ds(0, tail)], block_sem.at[1])
+
+            for s in range(groups, rounds):
+                spread(s)
+
+        def between():
+            arrived(centers.at[r, 0], relay_sem.at[r])
+
+        sides = (centers.at[r, core], centers.at[r, 1 - core])
+        nearest_of(emb, sides, half, best, accs, between)
         nearest[r] = jnp.maximum(norms[...] - 2.0 * best[...], 0.0) / float(width)
+
+    for q in range(2):
+        unused = accs[q][PIECES]
+        pltpu.matmul_acc_lhs(unused, jnp.zeros((NORM_ROWS, width), jnp.bfloat16), load_staged_rhs=0)
+        pltpu.matmul_pop(unused)
 
     load_prior.wait()
     current = prior[...]
@@ -330,7 +354,7 @@
     for r in range(rounds):
         current = jnp.minimum(current, nearest[r])
         own_rows[pl.ds(r, 1), :] = jnp.sum(current, axis=0, keepdims=True)
-    dist_ref[...] = current
+    both_ref[pl.ds(0, rows // LANES), :] = current
     sums = jnp.broadcast_to(jnp.sum(own_rows[...], axis=1, keepdims=True), (8, LANES))
     lane = lax.broadcasted_iota(jnp.int32, (8, LANES), 1)
     row = lax.broadcasted_iota(jnp.int32, (8, LANES), 0)
@@ -349,7 +373,8 @@
 
     totals[pl.ds(me, 1)] = own_total[...][None]
     arrived(totals.at[pl.ds(0, devs - 1)], total_sem)
-    mean_ref[...] = jnp.sum(totals[...], axis=0) / float(rows * devs)
+    mean = jnp.sum(totals[...], axis=0) / float(rows * devs)
+    both_ref[pl.ds(rows // LANES, 8), :] = jnp.broadcast_to(mean, (8, LANES))
 
     arrived(parts.at[0, pl.ds(0, devs - 1)], send_sem.at[0])
     arrived(blocks.at[pl.ds(0, groups - 1)], send_sem.at[2])
@@ -365,9 +390,10 @@
     arrived(totals.at[pl.ds(0, devs - 1)], send_sem.at[4 + 2 * rounds])
 
 
-def finish(dist_in, mean_in, dist_ref, mean_ref):
-    dist_ref[...] = dist_in[...]
-    mean_ref[...] = mean_in[:, : mean_ref.shape[1]]
+def finish(both, dist_ref, mean_ref):
+    count = dist_ref.shape[0]
+    dist_ref[...] = both[pl.ds(0, count), :]
+    mean_ref[...] = both[pl.ds(count, 1), : mean_ref.shape[1]]
 
 
 def body(embeddings, prior_dist, seed_ids):
@@ -380,26 +406,24 @@
     flat = (rows // LANES, LANES)
     vmem = pl.BlockSpec(memory_space=pltpu.VMEM)
     hbm = pl.BlockSpec(memory_space=pltpu.HBM)
-    dist, means = pl.pallas_call(
+    inputs = (seed_ids, embeddings, prior_dist.reshape(flat))
+    both = pl.pallas_call(
         functools.partial(kernel, sizes),
         name="seeding",
-        out_shape=(
-            jax.ShapeDtypeStruct(flat, jnp.float32),
-            jax.ShapeDtypeStruct((1, LANES), jnp.float32),
-        ),
+        out_shape=jax.ShapeDtypeStruct((rows // LANES + 8, LANES), jnp.float32),
         in_specs=[hbm, hbm, hbm],
-        out_specs=(vmem, vmem),
+        out_specs=vmem,
         scratch_shapes=[
             pltpu.SMEM((slots, seeds), jnp.int32),
             pltpu.VMEM((rows, width), jnp.bfloat16),
             pltpu.VMEM(flat, jnp.float32),
-            pltpu.VMEM((2 * rows + 16, LANES), jnp.float32),
+            pltpu.VMEM((2 * rows + 2 * EDGE, LANES), jnp.float32),
             pltpu.VMEM((2 * seeds, LANES), jnp.float32),
             pltpu.VMEM((slots, devs, share, width), jnp.bfloat16),
             pltpu.VMEM((slots, devs, share, width), jnp.bfloat16),
             pltpu.VMEM((rounds, share, width), jnp.bfloat16),
             pltpu.VMEM((rounds, 2, devs // 2, share, width), jnp.bfloat16),
-            pltpu.VMEM((seeds, LANES), jnp.float32),
+            pltpu.VMEM((2, seeds // 2, LANES), jnp.float32),
             pltpu.VMEM(flat, jnp.float32),
             pltpu.VMEM(flat, jnp.float32),
             pltpu.VMEM((rounds, *flat), jnp.float32),
@@ -417,9 +441,9 @@
             pltpu.SemaphoreType.DMA,
         ],
         compiler_params=pltpu.CompilerParams(
-            collective_id=0, has_side_effects=True, vmem_limit_bytes=67_000_000
+            collective_id=0, has_side_effects=True, vmem_limit_bytes=48 * 1024 * 1024
         ),
-    )(seed_ids, embeddings, prior_dist.reshape(flat))
+    )(*(pltpu.with_memory_space_constraint(x, pltpu.HBM) for x in inputs))
     dist, means = pl.pallas_call(
         finish,
         name="finish",
@@ -427,10 +451,10 @@
             jax.ShapeDtypeStruct(flat, jnp.float32),
             jax.ShapeDtypeStruct((1, rounds), jnp.float32),
         ),
-        in_specs=[vmem, vmem],
+        in_specs=[vmem],
         out_specs=(vmem, vmem),
         compiler_params=pltpu.CompilerParams(vmem_limit_bytes=1024 * 1024),
-    )(dist, means)
+    )(both)
     return dist.reshape(rows), means.reshape(rounds, 1)
 
 

time: 48.4 us -> 44.2 us (0.913)
  Pallas kernels: 46.2 us -> 43.5 us
  local copies, waits for them, and re-layouts: 1.35 us -> 0 us
    pallas_call x1, Pallas kernels: 45.6 us -> 42.8 us  [body(): pl.pallas_call(functools.partial(kernel, sizes), name='seeding', out_shap...]
    unnamed x4 -> x0, local copies, waits for them, and re-layouts: 1.35 us -> none
where the time goes in v4:
time: 44.2 us; the launch traced here: 44.1 us
  Pallas kernels  43.5 us (98%)
  between operations  0.64 us (1%)
    pallas_call x1, Pallas kernels, body(): pl.pallas_call(functools.partial(kernel, sizes), name='seeding', out_shap...  42.8 us

profile of v4, /device:TPU:1, one launch (start us, length us, event | category | flops | bytes accessed | tf_op | source)
XLA Modules:
  0.0 44.1 jit_solution(6522175536290491356)
XLA Ops:
  0.6 42.8 %seeding.1.both = f32[72,128]{1,0:T(8,128)S(1)} custom-call(s32[6,512]{1,0:T(8,128)} %refs_0_.1, bf16[8192,256]{1,0:T(8,128)(2,1)} %refs_1_.1, f32[64,128]{1,0:T(8,128)} %bitcast.3), custom_call_target="tpu_custom_call" | custom-call | tf_op jit(solution)/shard_map/seeding/pallas_call | solution.py:410
  43.5 0.6 %finish.1 = (f32[64,128]{1,0:T(8,128)}, f32[1,6]{1,0:T(1,128)}) custom-call(f32[72,128]{1,0:T(8,128)S(1)} %seeding.1.both), custom_call_target="tpu_custom_call" | custom-call | tf_op jit(solution)/shard_map/finish/pallas_call | solution.py:447

commit v5 on v4

--- a/solution.py
+++ b/solution.py
@@ -16,18 +16,21 @@
 LAG = 4
 EDGE = 8
 NORM_ROWS = 16
+NORM_PARTS = 2
 
 
 def tile_of(emb, j):
     return emb[pl.ds(pl.multiple_of(j * CHUNK, CHUNK), CHUNK), :]
 
 
-def row_norms(emb, norms, accs):
+def row_norms(emb, norms, accs, part):
     width = emb.shape[1]
     ones = jnp.ones((NORM_ROWS, width), jnp.bfloat16)
     steps = 4
 
-    @pl.loop(0, emb.shape[0] // CHUNK // (2 * steps))
+    trips = emb.shape[0] // CHUNK // (2 * steps)
+
+    @pl.loop(part * trips // NORM_PARTS, (part + 1) * trips // NORM_PARTS)
     def _(t):
         for i in range(steps):
             for q in range(2):
@@ -169,6 +172,7 @@
     pieces = load_sem.shape[0]
     piece = rows // pieces
     tail = rounds - groups
+    reach = (1, 3, 2)
 
     def load(k):
         return pltpu.make_async_copy(
@@ -214,35 +218,47 @@
             for h in range(2):
                 wide[pl.ds(EDGE + 2 * at + h, 128, stride=2), :] = x[:, h * LANES : (h + 1) * LANES]
 
-    def pick(slot):
+    def owner(q):
+        return lax.rem(me + 1 + q, devs)
+
+    def pick(slot, t):
+        for v in range(PICK // share):
+            to = owner(t * (PICK // share) + v)
+            row = pl.multiple_of(to * 2 * share, 2 * share)
+            for u in range(share):
+                at = jnp.clip(ids[slot, to * share + u] - base, -1, rows)
+                pick_wide[pl.ds(row + 2 * u, 2), :] = wide[pl.ds(2 * at + EDGE, 2), :]
+            for h in range(2):
+                picks[slot, to, :, h * LANES : (h + 1) * LANES] = pick_wide[
+                    pl.ds(row + h, share, stride=2), :
+                ].astype(jnp.bfloat16)
+
+    def send_pick(slot, q):
+        to = owner(q)
+        pltpu.make_async_remote_copy(
+            src_ref=picks.at[slot, to],
+            dst_ref=parts.at[slot, me],
+            send_sem=send_sem.at[slot],
+            recv_sem=part_sem.at[slot],
+            device_id={"dev": to},
+            device_id_type=MESH,
+        ).start()
+
+    def scatter(slot, entry=None):
         load_ids(slot).wait()
-
-        @pl.loop(0, seeds // PICK)
+        each = PICK // share
+        pick(slot, 0)
+        if entry is not None:
+            entry()
+
+        @pl.loop(1, devs // each)
         def _(t):
-            for u in range(PICK):
-                at = jnp.clip(ids[slot, t * PICK + u] - base, -1, rows)
-                pick_wide[pl.ds(2 * (t * PICK + u), 2), :] = wide[pl.ds(2 * at + EDGE, 2), :]
-
-        @pl.loop(0, devs, unroll=4)
-        def _(t):
-            for h in range(2):
-                picks[slot, t, :, h * LANES : (h + 1) * LANES] = pick_wide[
-                    pl.ds(2 * share * t + h, share, stride=2), :
-                ].astype(jnp.bfloat16)
-
-    def scatter(slot):
-        @pl.loop(1, devs)
-        def _(p):
-            to = lax.rem(me + p, devs)
-            pltpu.make_async_remote_copy(
-                src_ref=picks.at[slot, to],
-                dst_ref=parts.at[slot, me],
-                send_sem=send_sem.at[slot],
-                recv_sem=part_sem.at[slot],
-                device_id={"dev": to},
-                device_id_type=MESH,
-            ).start()
-
+            pick(slot, t)
+            for v in range(each):
+                send_pick(slot, (t - 1) * each + v)
+
+        for q in range(devs - each, devs - 1):
+            send_pick(slot, q)
         parts[slot, pl.ds(me, 1)] = picks[slot, pl.ds(me, 1)]
 
     def take(slot):
@@ -252,12 +268,12 @@
 
     def trade(slot):
         index = me_grp + groups * slot
-        for p in range(1, groups):
+        for p in reach:
             pltpu.make_async_remote_copy(
                 src_ref=blocks.at[index],
                 dst_ref=blocks.at[index],
                 send_sem=send_sem.at[2 + slot],
-                recv_sem=block_sem.at[slot],
+                recv_sem=block_sem.at[index],
                 device_id={"grp": lax.rem(me_grp + p, groups)},
                 device_id_type=MESH,
             ).start()
@@ -288,29 +304,26 @@
         ).start()
 
     def turn(i):
-        lap = i // groups
-        return lap * groups + lax.rem(me_grp * (1 - lap) + i, groups)
-
-    pick(0)
-    pl.semaphore_wait(barrier, devs - 1 + groups - 1)
-    scatter(0)
-    row_norms(emb, norms, accs)
+        lap, j = i // groups, lax.rem(i, groups)
+        ahead = j + j // 2 * (groups + 1 - 2 * j)
+        return lap * groups + lax.rem(me_grp * (1 - lap) + ahead, groups)
+
+    scatter(0, lambda: pl.semaphore_wait(barrier, devs - 1 + groups - 1))
 
     @pl.when(me_grp < tail)
     def _():
-        pick(1)
-
+        scatter(1)
+
+    row_norms(emb, norms, accs, 0)
     take(0)
     trade(0)
     spread(me_grp)
 
-    @pl.when(me_grp < tail)
-    def _():
-        scatter(1)
-
-    arrived(blocks.at[pl.ds(0, groups - 1)], block_sem.at[0])
-    for i in range(1, groups):
-        spread(turn(i))
+    row_norms(emb, norms, accs, 1)
+    for p in reach:
+        near = lax.rem(me_grp + p, groups)
+        arrived(blocks.at[near], block_sem.at[near])
+        spread(near)
     push_tiles(emb, 0)
 
     @pl.loop(0, rounds)
@@ -325,16 +338,13 @@
 
         @pl.when(i == 2)
         def _():
-            @pl.when(me_grp < tail)
-            def _():
-                arrived(blocks.at[pl.ds(0, tail - 1)], block_sem.at[1])
-
-            @pl.when(me_grp >= tail)
-            def _():
-                arrived(blocks.at[pl.ds(0, tail)], block_sem.at[1])
-
-            for s in range(groups, rounds):
-                spread(s)
+            for index in range(groups, rounds):
+
+                @pl.when(me_grp != index - groups)
+                def _():
+                    arrived(blocks.at[index], block_sem.at[index])
+
+                spread(index)
 
         def between():
             arrived(centers.at[r, 0], relay_sem.at[r])
@@ -435,7 +445,7 @@
             pltpu.SemaphoreType.DMA,
             pltpu.SemaphoreType.DMA((5 + 2 * rounds,)),
             pltpu.SemaphoreType.DMA((2,)),
-            pltpu.SemaphoreType.DMA((2,)),
+            pltpu.SemaphoreType.DMA((rounds,)),
             pltpu.SemaphoreType.DMA((rounds,)),
             pltpu.SemaphoreType.DMA((rounds,)),
             pltpu.SemaphoreType.DMA,

time: 44.2 us -> 43 us (0.973)
  Pallas kernels: 43.5 us -> 42.3 us
    pallas_call x1, Pallas kernels: 42.8 us -> 41.7 us  [body(): pl.pallas_call(functools.partial(kernel, sizes), name='seeding', out_shap...]
where the time goes in v5:
time: 43 us; the launch traced here: 42.9 us
  Pallas kernels  42.3 us (98%)
  between operations  0.64 us (1%)
    pallas_call x1, Pallas kernels, body(): pl.pallas_call(functools.partial(kernel, sizes), name='seeding', out_shap...  41.7 us

profile of v5, /device:TPU:1, one launch (start us, length us, event | category | flops | bytes accessed | tf_op | source)
XLA Modules:
  0.0 42.9 jit_solution(6288274141310372467)
XLA Ops:
  0.6 41.7 %seeding.1.both = f32[72,128]{1,0:T(8,128)S(1)} custom-call(s32[6,512]{1,0:T(8,128)} %refs_0_.1, bf16[8192,256]{1,0:T(8,128)(2,1)} %refs_1_.1, f32[64,128]{1,0:T(8,128)} %bitcast.3), custom_call_target="tpu_custom_call" | custom-call | tf_op jit(solution)/shard_map/seeding/pallas_call | solution.py:420
  42.3 0.6 %finish.1 = (f32[64,128]{1,0:T(8,128)}, f32[1,6]{1,0:T(1,128)}) custom-call(f32[72,128]{1,0:T(8,128)S(1)} %seeding.1.both), custom_call_target="tpu_custom_call" | custom-call | tf_op jit(solution)/shard_map/finish/pallas_call | solution.py:457

commit v6 on v5

--- a/solution.py
+++ b/solution.py
@@ -324,6 +324,12 @@
         near = lax.rem(me_grp + p, groups)
         arrived(blocks.at[near], block_sem.at[near])
         spread(near)
+
+    @pl.when(me_grp < tail)
+    def _():
+        take(1)
+        trade(1)
+
     push_tiles(emb, 0)
 
     @pl.loop(0, rounds)
@@ -331,12 +337,7 @@
         r = turn(i)
         relay(r)
 
-        @pl.when((i == 1) & (me_grp < tail))
-        def _():
-            take(1)
-            trade(1)
-
-        @pl.when(i == 2)
+        @pl.when(i == 1)
         def _():
             for index in range(groups, rounds):
 

time: 43 us -> 42.4 us (0.986)
  Pallas kernels: 42.3 us -> 41.7 us
    pallas_call x1, Pallas kernels: 41.7 us -> 41 us  [body(): pl.pallas_call(functools.partial(kernel, sizes), name='seeding', out_shap...]
where the time goes in v6:
time: 42.4 us; the launch traced here: 42.3 us
  Pallas kernels  41.7 us (98%)
  between operations  0.64 us (2%)
    pallas_call x1, Pallas kernels, body(): pl.pallas_call(functools.partial(kernel, sizes), name='seeding', out_shap...  41 us

profile of v6, /device:TPU:1, one launch (start us, length us, event | category | flops | bytes accessed | tf_op | source)
XLA Modules:
  0.0 42.3 jit_solution(939665044635755635)
XLA Ops:
  0.6 41.0 %seeding.1.both = f32[72,128]{1,0:T(8,128)S(1)} custom-call(s32[6,512]{1,0:T(8,128)} %refs_0_.1, bf16[8192,256]{1,0:T(8,128)(2,1)} %refs_1_.1, f32[64,128]{1,0:T(8,128)} %bitcast.3), custom_call_target="tpu_custom_call" | custom-call | tf_op jit(solution)/shard_map/seeding/pallas_call | solution.py:421
  41.7 0.6 %finish.1 = (f32[64,128]{1,0:T(8,128)}, f32[1,6]{1,0:T(1,128)}) custom-call(f32[72,128]{1,0:T(8,128)S(1)} %seeding.1.both), custom_call_target="tpu_custom_call" | custom-call | tf_op jit(solution)/shard_map/finish/pallas_call | solution.py:458

commit v7 on v6

--- a/solution.py
+++ b/solution.py
@@ -135,11 +135,15 @@
     prior_hbm,
     both_ref,
     ids,
+    places,
+    spots,
     emb,
     prior,
     wide,
     pick_wide,
     picks,
+    pair,
+    sums,
     parts,
     blocks,
     centers,
@@ -152,8 +156,10 @@
     totals,
     load_sem,
     id_sem,
+    place_sem,
     prior_sem,
     send_sem,
+    pair_sem,
     part_sem,
     block_sem,
     center_sem,
@@ -182,8 +188,15 @@
     def load_ids(slot):
         which = me_grp + groups * slot
         return pltpu.make_async_copy(
-            ids_hbm.at[pl.ds(which, 1)], ids.at[pl.ds(slot, 1)], id_sem.at[slot]
+            ids_hbm.at[pl.ds(which, 1)], ids.at[slot], id_sem.at[slot]
         )
+
+    def place(slot):
+        load_ids(slot).wait()
+        places[slot] = 2 * jnp.clip(ids[slot] - base, -1, rows) + EDGE
+
+    def move_places(slot):
+        return pltpu.make_async_copy(places.at[slot], spots[slot], place_sem.at[slot])
 
     load_ids(0).start()
     for k in range(pieces):
@@ -210,6 +223,19 @@
         wide[pl.ds(edge, EDGE), :] = jnp.zeros((EDGE, LANES), jnp.float32)
     for k in range(pieces):
         load(k).wait()
+        if k == 1:
+            place(0)
+
+            @pl.when(me_grp < tail)
+            def _():
+                place(1)
+
+        if k == pieces // 2:
+            move_places(0).start()
+
+            @pl.when(me_grp < tail)
+            def _():
+                move_places(1).start()
 
         @pl.loop(0, piece // 128)
         def _(t, k=k):
@@ -218,51 +244,63 @@
             for h in range(2):
                 wide[pl.ds(EDGE + 2 * at + h, 128, stride=2), :] = x[:, h * LANES : (h + 1) * LANES]
 
-    def owner(q):
-        return lax.rem(me + 1 + q, devs)
-
-    def pick(slot, t):
-        for v in range(PICK // share):
-            to = owner(t * (PICK // share) + v)
-            row = pl.multiple_of(to * 2 * share, 2 * share)
-            for u in range(share):
-                at = jnp.clip(ids[slot, to * share + u] - base, -1, rows)
-                pick_wide[pl.ds(row + 2 * u, 2), :] = wide[pl.ds(2 * at + EDGE, 2), :]
-            for h in range(2):
-                picks[slot, to, :, h * LANES : (h + 1) * LANES] = pick_wide[
-                    pl.ds(row + h, share, stride=2), :
-                ].astype(jnp.bfloat16)
-
-    def send_pick(slot, q):
-        to = owner(q)
+    def pick(slot, side):
+        each = PICK // share
+
+        @pl.loop(0, chips // each)
+        def _(t):
+            for v in range(each):
+                c = t * each + v
+                to = c * cores + side
+                row = pl.multiple_of(to * 2 * share, 2 * share)
+                for u in range(share):
+                    at = spots[slot][0, to * share + u]
+                    pick_wide[pl.ds(row + 2 * u, 2), :] = wide[pl.ds(at, 2), :]
+                for h in range(2):
+                    picks[slot, side, c, :, h * LANES : (h + 1) * LANES] = pick_wide[
+                        pl.ds(row + h, share, stride=2), :
+                    ].astype(jnp.bfloat16)
+
+    def pair_up(slot):
         pltpu.make_async_remote_copy(
-            src_ref=picks.at[slot, to],
-            dst_ref=parts.at[slot, me],
-            send_sem=send_sem.at[slot],
-            recv_sem=part_sem.at[slot],
-            device_id={"dev": to},
+            src_ref=picks.at[slot, 1 - core],
+            dst_ref=pair.at[slot],
+            send_sem=send_sem.at[5 + 2 * rounds + slot],
+            recv_sem=pair_sem.at[slot],
+            device_id={"dev": chip * cores + 1 - core},
             device_id_type=MESH,
         ).start()
 
-    def scatter(slot, entry=None):
-        load_ids(slot).wait()
-        each = PICK // share
-        pick(slot, 0)
-        if entry is not None:
-            entry()
-
-        @pl.loop(1, devs // each)
-        def _(t):
-            pick(slot, t)
-            for v in range(each):
-                send_pick(slot, (t - 1) * each + v)
-
-        for q in range(devs - each, devs - 1):
-            send_pick(slot, q)
-        parts[slot, pl.ds(me, 1)] = picks[slot, pl.ds(me, 1)]
+    def scatter(slot):
+        arrived(pair.at[slot], pair_sem.at[slot])
+
+        def add(q):
+            c = lax.rem(chip + 1 + q, chips)
+            total = picks[slot, core, c].astype(jnp.float32) + pair[slot, c].astype(jnp.float32)
+            sums[slot, c] = total.astype(jnp.bfloat16)
+
+        def send(q):
+            c = lax.rem(chip + 1 + q, chips)
+            pltpu.make_async_remote_copy(
+                src_ref=sums.at[slot, c],
+                dst_ref=parts.at[slot, chip],
+                send_sem=send_sem.at[slot],
+                recv_sem=part_sem.at[slot],
+                device_id={"dev": c * cores + core},
+                device_id_type=MESH,
+            ).start()
+
+        add(0)
+
+        @pl.loop(1, chips)
+        def _(q):
+            add(q)
+            send(q - 1)
+
+        parts[slot, chip] = sums[slot, chip]
 
     def take(slot):
-        arrived(parts.at[slot, pl.ds(0, devs - 1)], part_sem.at[slot])
+        arrived(parts.at[slot, pl.ds(0, chips - 1)], part_sem.at[slot])
         total = jnp.sum(parts[slot].astype(jnp.float32), axis=0)
         blocks[me_grp + groups * slot] = total.astype(jnp.bfloat16)
 
@@ -308,10 +346,23 @@
         ahead = j + j // 2 * (groups + 1 - 2 * j)
         return lap * groups + lax.rem(me_grp * (1 - lap) + ahead, groups)
 
-    scatter(0, lambda: pl.semaphore_wait(barrier, devs - 1 + groups - 1))
+    move_places(0).wait()
+    pick(0, 1 - core)
+    pl.semaphore_wait(barrier, devs - 1 + groups - 1)
+    pair_up(0)
 
     @pl.when(me_grp < tail)
     def _():
+        move_places(1).wait()
+        pick(1, 1 - core)
+        pair_up(1)
+
+    pick(0, core)
+    scatter(0)
+
+    @pl.when(me_grp < tail)
+    def _():
+        pick(1, core)
         scatter(1)
 
     row_norms(emb, norms, accs, 0)
@@ -387,12 +438,14 @@
     mean = jnp.sum(totals[...], axis=0) / float(rows * devs)
     both_ref[pl.ds(rows // LANES, 8), :] = jnp.broadcast_to(mean, (8, LANES))
 
-    arrived(parts.at[0, pl.ds(0, devs - 1)], send_sem.at[0])
+    arrived(parts.at[0, pl.ds(0, chips - 1)], send_sem.at[0])
+    arrived(pair.at[0], send_sem.at[5 + 2 * rounds])
     arrived(blocks.at[pl.ds(0, groups - 1)], send_sem.at[2])
 
     @pl.when(me_grp < tail)
     def _():
-        arrived(parts.at[1, pl.ds(0, devs - 1)], send_sem.at[1])
+        arrived(parts.at[1, pl.ds(0, chips - 1)], send_sem.at[1])
+        arrived(pair.at[1], send_sem.at[6 + 2 * rounds])
         arrived(blocks.at[pl.ds(0, groups - 1)], send_sem.at[3])
 
     for r in range(rounds):
@@ -425,13 +478,17 @@
         in_specs=[hbm, hbm, hbm],
         out_specs=vmem,
         scratch_shapes=[
-            pltpu.SMEM((slots, seeds), jnp.int32),
+            pltpu.VMEM((slots, 1, seeds), jnp.int32),
+            pltpu.VMEM((slots, 1, seeds), jnp.int32),
+            [pltpu.SMEM((1, seeds), jnp.int32)] * slots,
             pltpu.VMEM((rows, width), jnp.bfloat16),
             pltpu.VMEM(flat, jnp.float32),
             pltpu.VMEM((2 * rows + 2 * EDGE, LANES), jnp.float32),
             pltpu.VMEM((2 * seeds, LANES), jnp.float32),
-            pltpu.VMEM((slots, devs, share, width), jnp.bfloat16),
-            pltpu.VMEM((slots, devs, share, width), jnp.bfloat16),
+            pltpu.VMEM((slots, 2, devs // 2, share, width), jnp.bfloat16),
+            pltpu.VMEM((slots, devs // 2, share, width), jnp.bfloat16),
+            pltpu.VMEM((slots, devs // 2, share, width), jnp.bfloat16),
+            pltpu.VMEM((slots, devs // 2, share, width), jnp.bfloat16),
             pltpu.VMEM((rounds, share, width), jnp.bfloat16),
             pltpu.VMEM((rounds, 2, devs // 2, share, width), jnp.bfloat16),
             pltpu.VMEM((2, seeds // 2, LANES), jnp.float32),
@@ -443,8 +500,10 @@
             pltpu.VMEM((devs, 1, LANES), jnp.float32),
             pltpu.SemaphoreType.DMA((8,)),
             pltpu.SemaphoreType.DMA((slots,)),
+            pltpu.SemaphoreType.DMA((slots,)),
             pltpu.SemaphoreType.DMA,
-            pltpu.SemaphoreType.DMA((5 + 2 * rounds,)),
+            pltpu.SemaphoreType.DMA((7 + 2 * rounds,)),
+            pltpu.SemaphoreType.DMA((2,)),
             pltpu.SemaphoreType.DMA((2,)),
             pltpu.SemaphoreType.DMA((rounds,)),
             pltpu.SemaphoreType.DMA((rounds,)),

time: 42.4 us -> 41.4 us (0.976)
  Pallas kernels: 41.7 us -> 40.7 us
    pallas_call x1, Pallas kernels: 41 us -> 40.1 us  [body(): pl.pallas_call(functools.partial(kernel, sizes), name='seeding', out_shap...]
where the time goes in v7:
time: 41.4 us; the launch traced here: 41.3 us
  Pallas kernels  40.7 us (98%)
  between operations  0.64 us (2%)
    pallas_call x1, Pallas kernels, body(): pl.pallas_call(functools.partial(kernel, sizes), name='seeding', out_shap...  40.1 us

profile of v7, /device:TPU:1, one launch (start us, length us, event | category | flops | bytes accessed | tf_op | source)
XLA Modules:
  0.0 41.3 jit_solution(1021850477552186080)
XLA Ops:
  0.6 40.1 %seeding.1.both = f32[72,128]{1,0:T(8,128)S(1)} custom-call(s32[6,512]{1,0:T(8,128)} %refs_0_.1, bf16[8192,256]{1,0:T(8,128)(2,1)} %refs_1_.1, f32[64,128]{1,0:T(8,128)} %bitcast.3), custom_call_target="tpu_custom_call" | custom-call | tf_op jit(solution)/shard_map/seeding/pallas_call | solution.py:474
  40.7 0.6 %finish.1 = (f32[64,128]{1,0:T(8,128)}, f32[1,6]{1,0:T(1,128)}) custom-call(f32[72,128]{1,0:T(8,128)S(1)} %seeding.1.both), custom_call_target="tpu_custom_call" | custom-call | tf_op jit(solution)/shard_map/finish/pallas_call | solution.py:517

commit v8 on v7

--- a/solution.py
+++ b/solution.py
@@ -1,4 +1,5 @@
 import functools
+import math
 
 import jax
 import jax.numpy as jnp
@@ -13,6 +14,7 @@
 LANES = 128
 PIECE = 128
 PIECES = 7
+UNROLL = 3
 LAG = 4
 EDGE = 8
 NORM_ROWS = 16
@@ -65,49 +67,53 @@
     )
 
 
-def nearest_of(emb, sides, half, best, accs, between):
-    chips, share, width = sides[0].shape
-    trips = emb.shape[0] // CHUNK // 2
-    pieces = chips * share // PIECE
-    pending = []
-    run = {}
-
-    def pop():
-        unit, t, p, use = pending.pop(0)
-        offset = half[unit, pl.ds(p * PIECE, PIECE), :]
+class Stream:
+    def __init__(self, emb, half, accs):
+        self.emb, self.half, self.accs = emb, half, accs
+        self.pending = []
+        self.run = {}
+        self.count = 0
+        self.units = 0
+
+    def pop(self):
+        unit, side, best, t, p, pieces, use = self.pending.pop(0)
+        offset = self.half[unit, pl.ds(p * PIECE, PIECE), :]
         for q in range(2):
             value = pltpu.matmul_pop(use[q])
             for k in range(CHUNK // LANES):
                 short = value[:, k * LANES : (k + 1) * LANES] - offset
                 short = jnp.max(short.reshape(PIECE // 8, 8, LANES), axis=0)
-                run[q, k] = jnp.maximum(run[q, k], short) if p else short
+                self.run[q, k] = jnp.maximum(self.run[q, k], short) if p else short
         if p == pieces - 1:
-            for (q, k), value in list(run.items()):
+            for (q, k), value in list(self.run.items()):
                 row = (t * 2 + q) * (CHUNK // LANES) + k
                 value = jnp.max(value, axis=0, keepdims=True)
-                if unit:
+                if side:
                     value = jnp.maximum(value, best[pl.ds(row, 1), :])
                 best[pl.ds(row, 1), :] = value
 
-    count = 0
-    for unit in range(2):
-        if unit:
-            between()
-        half_norms(sides[unit], half, unit)
+    def side(self, center, side, best):
+        chips, share, width = center.shape
+        trips = self.emb.shape[0] // CHUNK // 2
+        pieces = chips * share // PIECE
+        half_norms(center, self.half, self.units)
         for t in range(trips):
             for p in range(pieces):
-                lhs = sides[unit][pl.ds(p * PIECE // share, PIECE // share)].reshape(PIECE, width)
-                use = [accs[q][count % PIECES] for q in range(2)]
-                count += 1
+                lhs = center[pl.ds(p * PIECE // share, PIECE // share)].reshape(PIECE, width)
+                use = [self.accs[q][self.count % PIECES] for q in range(2)]
+                self.count += 1
                 for q in range(2):
                     pltpu.matmul_acc_lhs(use[q], lhs, load_staged_rhs=None if p else 0)
                 if p == 0:
-                    push_tiles(emb, (t + 1) % trips)
-                pending.append((unit, t, p, use))
-                if len(pending) > LAG:
-                    pop()
-    while pending:
-        pop()
+                    push_tiles(self.emb, (t + 1) % trips)
+                self.pending.append((self.units, side, best, t, p, pieces, use))
+                if len(self.pending) > LAG:
+                    self.pop()
+        self.units += 1
+
+    def finish(self):
+        while self.pending:
+            self.pop()
 
 
 def kernel(sizes, *refs):
@@ -122,6 +128,12 @@
         run_kernel(sizes, *refs, (accs[:half], accs[half:]))
 
     pl.run_scoped(inner, *specs)
+
+
+def far_first(side):
+    ring = lambda d: min(d, side - d)
+    steps = [(a, b) for a in range(side) for b in range(side) if (a, b) != (0, 0)]
+    return sorted(steps, key=lambda s: -ring(s[0]) - ring(s[1]))
 
 
 def arrived(ref, sem):
@@ -149,7 +161,6 @@
     centers,
     half,
     norms,
-    best,
     nearest,
     own_rows,
     own_total,
@@ -174,12 +185,17 @@
     chips = devs // cores
     chip, core = me // cores, lax.rem(me, cores)
     base = (me_grp * devs + me) * rows
+    side = math.isqrt(chips)
     share = seeds // devs
     pieces = load_sem.shape[0]
     piece = rows // pieces
     tail = rounds - groups
     reach = (1, 3, 2)
 
+    def chip_at(step):
+        a, b = step
+        return lax.rem(chip // side + a, side) * side + lax.rem(chip + b, side)
+
     def load(k):
         return pltpu.make_async_copy(
             emb_hbm.at[pl.ds(k * piece, piece)], emb.at[pl.ds(k * piece, piece)], load_sem.at[k]
@@ -199,14 +215,15 @@
         return pltpu.make_async_copy(places.at[slot], spots[slot], place_sem.at[slot])
 
     load_ids(0).start()
+
+    @pl.when(me_grp < tail)
+    def _():
+        load_ids(1).start()
+
     for k in range(pieces):
         load(k).start()
     load_prior = pltpu.make_async_copy(prior_hbm, prior, prior_sem)
     load_prior.start()
-
-    @pl.when(me_grp < tail)
-    def _():
-        load_ids(1).start()
 
     barrier = pltpu.get_barrier_semaphore()
 
@@ -274,13 +291,11 @@
     def scatter(slot):
         arrived(pair.at[slot], pair_sem.at[slot])
 
-        def add(q):
-            c = lax.rem(chip + 1 + q, chips)
+        def add(c):
             total = picks[slot, core, c].astype(jnp.float32) + pair[slot, c].astype(jnp.float32)
             sums[slot, c] = total.astype(jnp.bfloat16)
 
-        def send(q):
-            c = lax.rem(chip + 1 + q, chips)
+        def send(c):
             pltpu.make_async_remote_copy(
                 src_ref=sums.at[slot, c],
                 dst_ref=parts.at[slot, chip],
@@ -290,13 +305,13 @@
                 device_id_type=MESH,
             ).start()
 
-        add(0)
-
-        @pl.loop(1, chips)
-        def _(q):
-            add(q)
-            send(q - 1)
-
+        order = [chip_at(step) for step in far_first(side)]
+        add(order[0])
+        for q in range(1, chips - 1):
+            add(order[q])
+            send(order[q - 1])
+        add(chip)
+        send(order[-1])
         parts[slot, chip] = sums[slot, chip]
 
     def take(slot):
@@ -317,14 +332,13 @@
             ).start()
 
     def spread(r):
-        @pl.loop(1, chips)
-        def _(p):
+        for step in far_first(side):
             pltpu.make_async_remote_copy(
                 src_ref=blocks.at[r],
                 dst_ref=centers.at[r, core, chip],
                 send_sem=send_sem.at[4 + r],
                 recv_sem=center_sem.at[r],
-                device_id={"dev": lax.rem(chip + p, chips) * cores + core},
+                device_id={"dev": chip_at(step) * cores + core},
                 device_id_type=MESH,
             ).start()
 
@@ -383,27 +397,28 @@
 
     push_tiles(emb, 0)
 
-    @pl.loop(0, rounds)
-    def _(i):
-        r = turn(i)
-        relay(r)
-
-        @pl.when(i == 1)
-        def _():
-            for index in range(groups, rounds):
-
-                @pl.when(me_grp != index - groups)
-                def _():
-                    arrived(blocks.at[index], block_sem.at[index])
-
-                spread(index)
-
-        def between():
+    @pl.loop(0, rounds // UNROLL)
+    def _(step):
+        stream = Stream(emb, half, accs)
+        for k in range(UNROLL):
+            i = step * UNROLL + k
+            r = turn(i)
+            relay(r)
+
+            @pl.when(i == 1)
+            def _():
+                for index in range(groups, rounds):
+
+                    @pl.when(me_grp != index - groups)
+                    def _():
+                        arrived(blocks.at[index], block_sem.at[index])
+
+                    spread(index)
+
+            stream.side(centers.at[r, core], 0, nearest.at[r])
             arrived(centers.at[r, 0], relay_sem.at[r])
-
-        sides = (centers.at[r, core], centers.at[r, 1 - core])
-        nearest_of(emb, sides, half, best, accs, between)
-        nearest[r] = jnp.maximum(norms[...] - 2.0 * best[...], 0.0) / float(width)
+            stream.side(centers.at[r, 1 - core], 1, nearest.at[r])
+        stream.finish()
 
     for q in range(2):
         unused = accs[q][PIECES]
@@ -414,7 +429,8 @@
     current = prior[...]
     own_rows[...] = jnp.zeros((8, LANES), jnp.float32)
     for r in range(rounds):
-        current = jnp.minimum(current, nearest[r])
+        gaps = jnp.maximum(norms[...] - 2.0 * nearest[r], 0.0) / float(width)
+        current = jnp.minimum(current, gaps)
         own_rows[pl.ds(r, 1), :] = jnp.sum(current, axis=0, keepdims=True)
     both_ref[pl.ds(0, rows // LANES), :] = current
     sums = jnp.broadcast_to(jnp.sum(own_rows[...], axis=1, keepdims=True), (8, LANES))
@@ -422,14 +438,14 @@
     row = lax.broadcasted_iota(jnp.int32, (8, LANES), 0)
     own_total[...] = jnp.sum(jnp.where(lane == row, sums, 0.0), axis=0, keepdims=True)
 
-    @pl.loop(1, devs)
-    def _(p):
+    peers = [chip_at(step) * cores + c for step in far_first(side) for c in range(cores)]
+    for peer in [*peers, chip * cores + 1 - core]:
         pltpu.make_async_remote_copy(
             src_ref=own_total,
             dst_ref=totals.at[me],
             send_sem=send_sem.at[4 + 2 * rounds],
             recv_sem=total_sem,
-            device_id={"dev": lax.rem(me + p, devs)},
+            device_id={"dev": peer},
             device_id_type=MESH,
         ).start()
 
@@ -491,8 +507,7 @@
             pltpu.VMEM((slots, devs // 2, share, width), jnp.bfloat16),
             pltpu.VMEM((rounds, share, width), jnp.bfloat16),
             pltpu.VMEM((rounds, 2, devs // 2, share, width), jnp.bfloat16),
-            pltpu.VMEM((2, seeds // 2, LANES), jnp.float32),
-            pltpu.VMEM(flat, jnp.float32),
+            pltpu.VMEM((2 * UNROLL, seeds // 2, LANES), jnp.float32),
             pltpu.VMEM(flat, jnp.float32),
             pltpu.VMEM((rounds, *flat), jnp.float32),
             pltpu.VMEM((8, LANES), jnp.float32),

time: 41.4 us -> 40.3 us (0.973)
  Pallas kernels: 40.7 us -> 39.6 us
    pallas_call x1, Pallas kernels: 40.1 us -> 38.9 us  [body(): pl.pallas_call(functools.partial(kernel, sizes), name='seeding', out_shap...]
where the time goes in v8:
time: 40.3 us; the launch traced here: 40.2 us
  Pallas kernels  39.6 us (98%)
  between operations  0.64 us (2%)
    pallas_call x1, Pallas kernels, body(): pl.pallas_call(functools.partial(kernel, sizes), name='seeding', out_shap...  38.9 us

profile of v8, /device:TPU:1, one launch (start us, length us, event | category | flops | bytes accessed | tf_op | source)
XLA Modules:
  0.0 40.2 jit_solution(9511733499622829570)
XLA Ops:
  0.6 38.9 %seeding.1.both = f32[72,128]{1,0:T(8,128)S(1)} custom-call(s32[6,512]{1,0:T(8,128)} %refs_0_.1, bf16[8192,256]{1,0:T(8,128)(2,1)} %refs_1_.1, f32[64,128]{1,0:T(8,128)} %bitcast.3), custom_call_target="tpu_custom_call" | custom-call | tf_op jit(solution)/shard_map/seeding/pallas_call | solution.py:490
  39.6 0.6 %finish.1 = (f32[64,128]{1,0:T(8,128)}, f32[1,6]{1,0:T(1,128)}) custom-call(f32[72,128]{1,0:T(8,128)S(1)} %seeding.1.both), custom_call_target="tpu_custom_call" | custom-call | tf_op jit(solution)/shard_map/finish/pallas_call | solution.py:532

commit v9 on v8

--- a/solution.py
+++ b/solution.py
@@ -14,7 +14,7 @@
 LANES = 128
 PIECE = 128
 PIECES = 7
-UNROLL = 3
+UNROLL = 6
 LAG = 4
 EDGE = 8
 NORM_ROWS = 16
@@ -227,9 +227,10 @@
 
     barrier = pltpu.get_barrier_semaphore()
 
-    @pl.loop(1, devs)
-    def _(p):
-        pl.semaphore_signal(barrier, inc=1, device_id={"dev": lax.rem(me + p, devs)}, device_id_type=MESH)
+    peers = [chip_at(step) * cores + c for step in far_first(side) for c in range(cores)]
+    peers.append(chip * cores + 1 - core)
+    for peer in peers:
+        pl.semaphore_signal(barrier, inc=1, device_id={"dev": peer}, device_id_type=MESH)
 
     for p in range(1, groups):
         pl.semaphore_signal(
@@ -438,8 +439,7 @@
     row = lax.broadcasted_iota(jnp.int32, (8, LANES), 0)
     own_total[...] = jnp.sum(jnp.where(lane == row, sums, 0.0), axis=0, keepdims=True)
 
-    peers = [chip_at(step) * cores + c for step in far_first(side) for c in range(cores)]
-    for peer in [*peers, chip * cores + 1 - core]:
+    for peer in peers:
         pltpu.make_async_remote_copy(
             src_ref=own_total,
             dst_ref=totals.at[me],

time: 40.3 us -> 40.3 us (level)
  no operation moved by 1% of the time
where the time goes in v9:
time: 40.3 us; the launch traced here: 40.2 us
  Pallas kernels  39.6 us (98%)
  between operations  0.64 us (2%)
    pallas_call x1, Pallas kernels, body(): pl.pallas_call(functools.partial(kernel, sizes), name='seeding', out_shap...  39 us

profile of v9, /device:TPU:1, one launch (start us, length us, event | category | flops | bytes accessed | tf_op | source)
XLA Modules:
  0.0 40.2 jit_solution(10082966070648057286)
XLA Ops:
  0.6 39.0 %seeding.1.both = f32[72,128]{1,0:T(8,128)S(1)} custom-call(s32[6,512]{1,0:T(8,128)} %refs_0_.1, bf16[8192,256]{1,0:T(8,128)(2,1)} %refs_1_.1, f32[64,128]{1,0:T(8,128)} %bitcast.3), custom_call_target="tpu_custom_call" | custom-call | tf_op jit(solution)/shard_map/seeding/pallas_call | solution.py:490
  39.6 0.6 %finish.1 = (f32[64,128]{1,0:T(8,128)}, f32[1,6]{1,0:T(1,128)}) custom-call(f32[72,128]{1,0:T(8,128)S(1)} %seeding.1.both), custom_call_target="tpu_custom_call" | custom-call | tf_op jit(solution)/shard_map/finish/pallas_call | solution.py:532
